TPU v7x, 128 devices: a whole 4x4x4 slice. The times are simulated.
128 devices in a mesh: member: 8 (over y, core), shard: 16 (over z, x).
Axes of the slice: x: 4, y: 4, z: 4, core: 2. Of those that a mesh axis runs over, the one named last changes fastest.
Arguments:
- member_grams: float32 [8, 4096, 4096], P('member', 'shard'), as said below
- member_weights: bfloat16 [8, 4096, 2304], P('member', 'shard'), may hold values from -6 to 6
Outputs:
- merged: float32 [4096, 2304], P('shard', 'member')
Inputs may be any that keep to these rules, and one draw needn't show every extreme that they name: `member_grams`: each member's matrix is symmetric positive definite.
All inputs are finite; a program needn't handle non-finite values.
Results may differ from a plain program's by a relative error of at most 0.0032.
Values may be sent and summed in bfloat16 or wider, within the bound.
No kernel may reach another device: no remote copies, remote signals or barrier semaphores. Data moves between devices by JAX's collectives and lax.ppermute only.
A program may use at most 128 MiB of HBM per device.

v0:
```python
import jax
import jax.numpy as jnp
from jax import lax
from jax.experimental import pallas as pl
from jax.experimental.pallas import tpu as pltpu
from jax.sharding import Mesh, PartitionSpec as P

MEMBER = ("y", "core")
SHARD = ("z", "x")
ALL = ("y", "core", "z", "x")
SIZES = (4, 2, 4, 4)
SHRINK = 0.9
ROWS = 256
CHUNK = 512
COLS = 144
PIECES = (64, 80)
SPARE = 16
FULL = ROWS + SPARE
F32 = jnp.float32
BF16 = jnp.bfloat16
VMEM = pl.BlockSpec(memory_space=pltpu.VMEM)
SMEM = pl.BlockSpec(memory_space=pltpu.SMEM)
HBM = pl.BlockSpec(memory_space=pltpu.HBM)
LIMIT = pltpu.CompilerParams(vmem_limit_bytes=16 * 2**20)


def exchange(parts, axis):
    return lax.all_to_all(parts, axis, split_axis=0, concat_axis=0, tiled=True)


def turn(block, axis, step):
    size = lax.axis_size(axis)
    return lax.ppermute(block, axis, [(i, (i + step) % size) for i in range(size)])


def dot(a, b):
    return jnp.dot(a, b, preferred_element_type=F32)


def cost(flops, moved):
    return pl.CostEstimate(flops=flops, bytes_accessed=moved, transcendentals=0)


def spare_rows(first, second):
    index = lax.broadcasted_iota(jnp.int32, (SPARE, first.shape[-1]), 0)
    return jnp.where(index == 0, first, jnp.where(index == 1, second, 0.0)).astype(BF16)


def transposed(weights):
    blocks = weights.shape[1] // COLS
    group = 8

    def body(w_ref, *out_refs):
        turned = w_ref[...].astype(F32).T.astype(BF16)
        for b in range(group):
            at = b * COLS
            for out_ref, piece in zip(out_refs, PIECES):
                out_ref[b * piece : (b + 1) * piece] = turned[at : at + piece]
                at += piece

    return pl.pallas_call(
        body,
        grid=(blocks // group,),
        in_specs=[pl.BlockSpec((ROWS, group * COLS), lambda i: (0, i))],
        out_specs=[pl.BlockSpec((group * p, ROWS), lambda i: (i, 0)) for p in PIECES],
        out_shape=[jax.ShapeDtypeStruct((blocks * p, ROWS), BF16) for p in PIECES],
        cost_estimate=cost(10**8, 2 * weights.size * 2),
        name="turn_weights",
    )(weights)


def spread_kernel(pos_ref, gram_ref, out_ref):
    for c in range(out_ref.shape[0]):
        gram = gram_ref[:, c * CHUNK : (c + 1) * CHUNK]
        first = (pl.program_id(0) * out_ref.shape[0] + c) * CHUNK
        row = lax.broadcasted_iota(jnp.int32, gram.shape, 0) + pos_ref[3] * ROWS
        col = lax.broadcasted_iota(jnp.int32, gram.shape, 1) + first
        on = row == col
        regular = jnp.where(on, gram, SHRINK * gram)
        low = regular.astype(BF16)
        rest = jnp.sum(jnp.where(on, regular - low.astype(F32), 0.0), axis=0, keepdims=True)
        out_ref[c, :ROWS] = low
        out_ref[c, ROWS:] = spare_rows(rest, jnp.zeros_like(rest))


def spread_grams(pos, gram):
    chunks = gram.shape[1] // CHUNK
    return pl.pallas_call(
        spread_kernel,
        grid=(chunks // 2,),
        in_specs=[SMEM, pl.BlockSpec((ROWS, 2 * CHUNK), lambda i: (0, i))],
        out_specs=pl.BlockSpec((2, FULL, CHUNK), lambda i: (i, 0, 0)),
        out_shape=jax.ShapeDtypeStruct((chunks, FULL, CHUNK), BF16),
        compiler_params=LIMIT,
        cost_estimate=cost(10**8, gram.size * 6),
        name="spread_grams",
    )(pos, gram)


def sum_kernel(pos_ref, blocks_ref, out_ref):
    total = jnp.sum(blocks_ref[...].astype(F32), axis=0)
    block, rest = total[:ROWS], total[ROWS : ROWS + 1]
    row = lax.broadcasted_iota(jnp.int32, block.shape, 0) + pos_ref[3] * ROWS
    col = lax.broadcasted_iota(jnp.int32, block.shape, 1) + pos_ref[4] * CHUNK
    on = row == col
    low = block.astype(BF16)
    kept = low.astype(F32)
    diag = jnp.sum(jnp.where(on, kept, 0.0), axis=0, keepdims=True)
    rest = rest + jnp.sum(jnp.where(on, block - kept, 0.0), axis=0, keepdims=True)
    out_ref[:ROWS] = low
    out_ref[ROWS:] = spare_rows(diag, rest)


def sum_grams(pos, blocks):
    return pl.pallas_call(
        sum_kernel,
        in_specs=[SMEM, VMEM],
        out_specs=VMEM,
        out_shape=jax.ShapeDtypeStruct((FULL, CHUNK), BF16),
        compiler_params=LIMIT,
        cost_estimate=cost(10**8, blocks.size * 2),
        name="sum_grams",
    )(pos, blocks)


def gather_weights(piece):
    middle = piece.shape[0] // 2
    up, down = turn(piece, "y", 1), turn(piece, "y", 3)
    far = [turn(up[:middle], "y", 1), turn(down[middle:], "y", 3)]
    mine = [piece, up, down] + far
    return mine + [turn(b, "core", 1) for b in mine]


def right_side_kernel(pos_ref, g_ref, *refs):
    blocks, out_ref = refs[:-1], refs[-1]
    y, core = pos_ref[0], pos_ref[1]
    grams = []
    for other in range(2):
        for step in (0, 3, 1, 2):
            grams.append(g_ref.at[2 * lax.rem(y + step, 4) + (1 - core if other else core)])
    middle = out_ref.shape[0] // 2
    for part in range(2):
        rows = slice(part * middle, (part + 1) * middle)
        total = jnp.zeros((middle, out_ref.shape[1]), F32)
        for other in range(2):
            five = blocks[5 * other : 5 * other + 5]
            for k in range(3):
                total += dot(five[k][rows], grams[4 * other + k][:ROWS])
            total += dot(five[3 + part][...], grams[4 * other + 3][:ROWS])
        out_ref[rows] = total.astype(BF16)


def right_side_part(pos, grams, blocks):
    rows = blocks[0].shape[0]
    return pl.pallas_call(
        right_side_kernel,
        in_specs=[SMEM, VMEM] + [VMEM] * len(blocks),
        out_specs=VMEM,
        out_shape=jax.ShapeDtypeStruct((rows, CHUNK), BF16),
        compiler_params=LIMIT,
        cost_estimate=cost(2 * rows * CHUNK * ROWS * 8, rows * ROWS * 16 + grams.size * 2 + rows * CHUNK * 2),
        name="right_side",
    )(pos, grams, *blocks)


def gather(block):
    mine = [block] + [turn(block, "y", step) for step in (1, 2, 3)]
    return mine + [turn(b, "core", 1) for b in mine]


def fetch(pos_ref, gram_hbm, parts, gram_ref, all_ref, sems):
    y, core = pos_ref[0], pos_ref[1]
    copies = []
    for i, part in enumerate(parts):
        at = lax.rem(y + 4 - i % 4, 4) * 2 + (core if i < 4 else 1 - core)
        copies.append(pltpu.make_async_copy(part, all_ref.at[at], sems.at[i]))
    grams = []
    for i in range(4):
        some = pl.ds(4 * i, 4)
        grams.append(pltpu.make_async_copy(gram_hbm.at[some], gram_ref.at[some], sems.at[8 + i]))
    for copy in copies + grams:
        copy.start()
    for copy in copies:
        copy.wait()
    return 2 * y + core, grams


def product(gram_ref, all_ref, at, grams, own):
    total = jnp.zeros(own.shape, F32)
    spare = jnp.zeros((8, CHUNK), F32)
    for s in range(16):
        if s % 4 == 0:
            grams[s // 4].wait()
        h = s % 2
        total += dot(all_ref[s // 2, :COLS, h * ROWS : (h + 1) * ROWS], gram_ref[s, :ROWS])
        spare += gram_ref[s, ROWS:].astype(F32)[:8]
    return total + spare[0:1] * (own - all_ref[at, :COLS].astype(F32)) + spare[1:2] * own


def own_sum(a, b):
    ones = jnp.ones((8, CHUNK), F32)
    return lax.dot_general(
        ones, a * b, (((1,), (1,)), ((), ())), precision=lax.Precision.HIGHEST, preferred_element_type=F32
    )


def put(out_ref, block, first, second):
    out_ref[:COLS] = block.astype(BF16)
    index = lax.broadcasted_iota(jnp.int32, (16, COLS), 0)
    rows = jnp.zeros((16, COLS), F32)
    for i, own in enumerate((first, second)):
        left = own[0:1]
        for j in range(3):
            top = left.astype(BF16).astype(F32)
            rows = jnp.where(index == 3 * i + j, top, rows)
            left = left - top
    out_ref[COLS:] = jnp.concatenate([rows, jnp.zeros((16, CHUNK - COLS), F32)], axis=1).astype(BF16)


def take(all_ref):
    rows = jnp.sum(all_ref[:, COLS:].astype(F32), axis=0)
    out = []
    for i in range(2):
        row = rows[3 * i : 3 * i + 1] + (rows[3 * i + 1 : 3 * i + 2] + rows[3 * i + 2 : 3 * i + 3])
        out.append(jnp.broadcast_to(row[:, :256], (128, 256)).T[:COLS, :1])
    return out


def wide(column):
    return jnp.broadcast_to(column, (column.shape[0], 128))


def first_kernel(times, sums, own_refs, outs):
    r0 = own_refs[0][...]
    w_ref, send_ref = outs
    w0 = times(r0)
    w_ref[...] = w0
    put(send_ref, w0, own_sum(r0, r0), own_sum(r0, w0))


def second_kernel(times, sums, own_refs, outs):
    r0, w0 = (ref[...] for ref in own_refs)
    z_ref, r1_ref, w1_ref, send_ref = outs
    norm0, curve0 = sums()
    step0 = norm0 / curve0
    z0 = times(w0)
    r1 = r0 - step0 * w0
    w1 = w0 - step0 * z0
    z_ref[:, :CHUNK] = z0
    z_ref[:, CHUNK : CHUNK + 128] = wide(norm0)
    z_ref[:, CHUNK + 128 :] = wide(step0)
    r1_ref[...] = r1
    w1_ref[...] = w1
    put(send_ref, w1, own_sum(r1, r1), own_sum(r1, w1))


def third_kernel(times, sums, own_refs, outs):
    r0, w0, z0, r1, w1 = (ref[...] for ref in own_refs)
    x_ref, r2_ref, p_ref, sums_ref = outs
    norm0, step0 = z0[:, CHUNK : CHUNK + 1], z0[:, CHUNK + 128 : CHUNK + 129]
    z0 = z0[:, :CHUNK]
    norm1, curve1 = sums()
    beta1 = norm1 / norm0
    step1 = norm1 / (curve1 - beta1 * norm1 / step0)
    p1 = r1 + beta1 * r0
    r2 = r1 - step1 * (w1 + beta1 * w0)
    x_ref[...] = step0 * r0 + step1 * p1
    r2_ref[...] = r2
    p_ref[:, :CHUNK] = p1
    p_ref[:, CHUNK : CHUNK + 128] = wide(norm1)
    p_ref[:, CHUNK + 128 :] = wide(step1)
    norm2 = own_sum(r2, r2)
    w2 = w1 - step1 * (times(w1) + beta1 * z0)
    sums_ref[...] = jnp.concatenate([norm2, own_sum(r2, w2)], axis=1)


def run(body, outs, gram_sum, parts, pos, *owns):
    rows = parts[0].shape[0]

    def kernel(pos_ref, *refs):
        own_refs, gram_hbm, part_refs = refs[: len(owns)], refs[len(owns)], refs[len(owns) + 1 : len(owns) + 9]
        out_refs, (gram_ref, all_ref, sems) = refs[len(owns) + 9 : -3], refs[-3:]
        at, grams = fetch(pos_ref, gram_hbm, part_refs, gram_ref, all_ref, sems)
        body(lambda own: product(gram_ref, all_ref, at, grams, own), lambda: take(all_ref), own_refs, out_refs)

    return pl.pallas_call(
        kernel,
        in_specs=[SMEM] + [VMEM] * len(owns) + [HBM] * (1 + len(parts)),
        out_specs=[VMEM] * len(outs),
        out_shape=outs,
        scratch_shapes=[
            pltpu.VMEM(gram_sum.shape, BF16),
            pltpu.VMEM((8, rows, CHUNK), BF16),
            pltpu.SemaphoreType.DMA((12,)),
        ],
        compiler_params=LIMIT,
        cost_estimate=cost(2 * COLS * CHUNK * 4096, 4096 * CHUNK * 2),
    )(pos, *owns, gram_sum, *parts)


def to_output(block):
    index = lambda y, core, z, x: ((y * 2 + core) * 4 + z) * 4 + x
    places = [(y, c, z, x) for y in range(4) for c in range(2) for z in range(4) for x in range(4)]
    odd = lax.axis_index("x") % 2
    halves = [block[:, :ROWS], block[:, ROWS:]]
    came = []
    for a in range(2):
        pairs = [
            (index(y, c, z, x), index(z, x // 2, y, 2 * c + ((x % 2) ^ a))) for y, c, z, x in places
        ]
        sent = jnp.where(odd == a, halves[0], halves[1])
        came.append(lax.ppermute(sent, ALL, pairs))
    first = jnp.where(odd == 0, came[0], came[1])
    second = jnp.where(odd == 0, came[1], came[0])
    return jnp.concatenate([first, second], axis=0).T


def shards(member_grams, member_weights):
    place = lax.axis_index(SHARD)
    chunk = lax.axis_index(MEMBER)
    pos = [lax.axis_index("y"), lax.axis_index("core"), 0, place, chunk, lax.axis_index("z"), lax.axis_index("x"), 0]
    pos = jnp.stack([jnp.asarray(p, jnp.int32) for p in pos])

    pieces = transposed(member_weights[0])
    early = gather_weights(pieces[0])
    ready, pieces = lax.optimization_barrier((pos, pieces))
    spread = spread_grams(ready, member_grams[0])
    grams = exchange(spread, MEMBER)
    late, grams = lax.optimization_barrier((pieces[1], grams))
    late = gather_weights(late)
    gram_sum = lax.all_gather(sum_grams(pos, grams), SHARD, axis=0)
    parts = []
    for piece, blocks in zip(PIECES, (early, late)):
        part = right_side_part(pos, grams, blocks)
        part = exchange(part.reshape(16, piece, CHUNK), SHARD)
        parts.append(jnp.sum(part.astype(F32), axis=0))
    r0 = jnp.concatenate(parts, axis=0)

    array = jax.ShapeDtypeStruct((COLS, CHUNK), F32)
    more = jax.ShapeDtypeStruct((COLS, CHUNK + 256), F32)
    sent = jax.ShapeDtypeStruct((COLS + 16, CHUNK), BF16)
    sums = jax.ShapeDtypeStruct((8, 2 * COLS), F32)
    w0, low = run(first_kernel, (array, sent), gram_sum, gather(r0.astype(BF16)), pos, r0)
    outs = (more, array, array, sent)
    z0, r1, w1, low = run(second_kernel, outs, gram_sum, gather(low), pos, r0, w0)
    outs = (array, array, more, sums)
    x1, r2, p1, both = run(third_kernel, outs, gram_sum, gather(low), pos, r0, w0, z0, r1, w1)
    norm1, step1 = p1[:, CHUNK : CHUNK + 1], p1[:, CHUNK + 128 : CHUNK + 129]
    p1 = p1[:, :CHUNK]
    both = jnp.sum(exchange(both.reshape(8, 1, 2 * COLS), MEMBER), axis=(0, 1))
    norm2, curve2 = both[:COLS, None], both[COLS:, None]
    beta2 = norm2 / norm1
    step2 = norm2 / (curve2 - beta2 * norm2 / step1)
    p2 = r2 + beta2 * p1
    return to_output(x1 + step2 * p2)


def solution(mesh):
    fine = Mesh(mesh.devices.reshape(SIZES), ALL)

    return jax.shard_map(
        shards,
        mesh=fine,
        in_specs=(P(MEMBER, SHARD, None), P(MEMBER, SHARD, None)),
        out_specs=P(SHARD, MEMBER),
        check_vma=False,
    )
```

profile of v0, /device:TPU:24, one launch (start us, length us, event | category | flops | bytes accessed | tf_op | source)
XLA Modules:
  0.0 231.3 jit_solution(13797283206151354356)
XLA Ops:
  6.5 2.4 %turn_weights.1 = (bf16[1024,256]{1,0:T(8,128)(2,1)}, bf16[1280,256]{1,0:T(8,128)(2,1)}) custom-call(bf16[256,2304]{1,0:T(8,128)(2,1)} %bitcast.21), custom_call_target="tpu_custom_call" | custom-call | flops 100000000 | bytes 2359296 | tf_op jit(solution)/shard_map/turn_weights/pallas_call | solution.py:61
  9.1 2.2 copy-done.1
  13.3 31.0 %all_to_all.20.g_ref.blocks_ref = bf16[8,272,512]{2,1,0:T(8,128)(2,1)S(1)} all-to-all(bf16[8,272,512]{2,1,0:T(8,128)(2,1)S(1)} %spread_grams.1), channel_id=1, replica_groups=mesh['y'=4,'core'=2,'z'=4,'x'=4] {'y','core'}, dimensions={0} | all-to-all | bytes 4456448 | tf_op jit(solution)/shard_map/all_to_all | solution.py:28
  48.2 11.4 %collective-permute-done.refs_1_ = bf16[1024,256]{1,0:T(8,128)(2,1)S(1)} collective-permute-done((bf16[1024,256]{1,0:T(8,128)(2,1)S(1)}, bf16[1024,256]{1,0:T(8,128)(2,1)S(1)}, u32[]{:S(2)}, u32[]{:S(2)}) %collective-permute-start) | collective-permute-done | bytes 524320 | tf_op jit(solution)/shard_map/ppermute | solution.py:33
  59.6 3.4 %collective-permute-start.2 = (bf16[512,256]{1,0:T(8,128)(2,1)S(1)}, bf16[512,256]{1,0:T(8,128)(2,1)S(1)}, u32[]{:S(2)}, u32[]{:S(2)}) collective-permute-start(bf16[512,256]{1,0:T(8,128)(2,1)S(1)} %slice.44), channel_id=1, source_target_pairs={{0,32},{32,64},{64,96},{96,0},{1,33},{33,65},{65,97},{97,1},{2,34}... | collective-permute-start | bytes 786440 | tf_op jit(solution)/shard_map/ppermute | solution.py:33
  63.1 4.4 %collective-permute-done.2.refs_3_ = bf16[512,256]{1,0:T(8,128)(2,1)S(1)} collective-permute-done((bf16[512,256]{1,0:T(8,128)(2,1)S(1)}, bf16[512,256]{1,0:T(8,128)(2,1)S(1)}, u32[]{:S(2)}, u32[]{:S(2)}) %collective-permute-start.2) | collective-permute-done | bytes 262176 | tf_op jit(solution)/shard_map/ppermute | solution.py:33
  68.0 3.7 %collective-permute-start.9 = (bf16[1280,256]{1,0:T(8,128)(2,1)}, bf16[1280,256]{1,0:T(8,128)(2,1)S(1)}, u32[]{:S(2)}, u32[]{:S(2)}) collective-permute-start(bf16[1280,256]{1,0:T(8,128)(2,1)} %get-tuple-element.26.refs_0_), channel_id=1, source_target_pairs={{0,32},{32,64},{64,96},{96,0},{1,33},{33,65},{65,97},{97,1},{2,34}... | collective-permute-start | bytes 1966088 | tf_op jit(solution)/shard_map/ppermute | solution.py:33
  74.4 3.9 %right_side.2 = bf16[1024,512]{1,0:T(8,128)(2,1)} custom-call(s32[8]{0:T(128)S(1)} %stack.27.pos_ref, bf16[8,272,512]{2,1,0:T(8,128)(2,1)S(1)} %all_to_all.20.g_ref.blocks_ref, bf16[1024,256]{1,0:T(8,128)(2,1)S(1)} %copy-done.3, bf16[1024,256]{1,0:T(8,128)(2,1)S(1)} %collective-permute-done.refs_1_, bf16[1024,256]{1,0:T(8,128)(2,1)S(1)} %collective-permute-done.1.refs_2_, ...), custom_call_target="tpu_custom_call" | custom-call | flops 2147483648 | bytes 7471104 | tf_op jit(solution)/shard_map/right_side/pallas_call | solution.py:155
  78.3 7.9 %all-to-all-start.1 = ((bf16[16,64,512]{2,1,0:T(8,128)(2,1)}), bf16[16,64,512]{2,1,0:T(8,128)(2,1)}, u32[]{:S(2)}, u32[]{:S(2)}) async-start(bf16[16,64,512]{2,1,0:T(8,128)(2,1)} %bitcast.8), calls=%async_computation.1 | async-start | bytes 2097152 | tf_op jit(solution)/shard_map/all_to_all | solution.py:28
  86.7 3.7 %collective-permute-start.11 = (bf16[640,256]{1,0:T(8,128)(2,1)S(1)}, bf16[640,256]{1,0:T(8,128)(2,1)S(1)}, u32[]{:S(2)}, u32[]{:S(2)}) collective-permute-start(bf16[640,256]{1,0:T(8,128)(2,1)S(1)} %slice.46), channel_id=1, source_target_pairs={{0,32},{32,64},{64,96},{96,0},{1,33},{33,65},{65,97},{97,1},{2,34}... | collective-permute-start | bytes 983048 | tf_op jit(solution)/shard_map/ppermute | solution.py:33
  91.1 6.2 %collective-permute-done.11.refs_3_ = bf16[640,256]{1,0:T(8,128)(2,1)S(1)} collective-permute-done((bf16[640,256]{1,0:T(8,128)(2,1)S(1)}, bf16[640,256]{1,0:T(8,128)(2,1)S(1)}, u32[]{:S(2)}, u32[]{:S(2)}) %collective-permute-start.11) | collective-permute-done | bytes 327712 | tf_op jit(solution)/shard_map/ppermute | solution.py:33
  97.3 3.5 %collective-permute-done.12.refs_4_ = bf16[640,256]{1,0:T(8,128)(2,1)S(1)} collective-permute-done((bf16[640,256]{1,0:T(8,128)(2,1)S(1)}, bf16[640,256]{1,0:T(8,128)(2,1)S(1)}, u32[]{:S(2)}, u32[]{:S(2)}) %collective-permute-start.12) | collective-permute-done | bytes 327712 | tf_op jit(solution)/shard_map/ppermute | solution.py:33
  102.4 5.1 %right_side.3 = bf16[1280,512]{1,0:T(8,128)(2,1)} custom-call(s32[8]{0:T(128)S(1)} %stack.27.pos_ref, bf16[8,272,512]{2,1,0:T(8,128)(2,1)S(1)} %all_to_all.20.g_ref.blocks_ref, bf16[1280,256]{1,0:T(8,128)(2,1)} %get-tuple-element.26.refs_0_, bf16[1280,256]{1,0:T(8,128)(2,1)S(1)} %collective-permute-done.9.refs_1_, ...), custom_call_target="tpu_custom_call" | custom-call | flops 2684354560 | bytes 8781824 | tf_op jit(solution)/shard_map/right_side/pallas_call | solution.py:155
  107.5 6.6 %all-to-all-done.1 = bf16[16,64,512]{2,1,0:T(8,128)(2,1)} async-done(((bf16[16,64,512]{2,1,0:T(8,128)(2,1)}), bf16[16,64,512]{2,1,0:T(8,128)(2,1)}, u32[]{:S(2)}, u32[]{:S(2)}) %all-to-all-start.1) | async-done | bytes 1048608 | tf_op jit(solution)/shard_map/all_to_all | solution.py:28
  114.1 3.7 %all-to-all-start.2 = ((bf16[16,80,512]{2,1,0:T(8,128)(2,1)}), bf16[16,80,512]{2,1,0:T(8,128)(2,1)S(1)}, u32[]{:S(2)}, u32[]{:S(2)}) async-start(bf16[16,80,512]{2,1,0:T(8,128)(2,1)} %bitcast.9), calls=%async_computation.2 | async-start | bytes 2621440 | tf_op jit(solution)/shard_map/all_to_all | solution.py:28
  119.2 20.0 %all-to-all-done.2 = bf16[16,80,512]{2,1,0:T(8,128)(2,1)S(1)} async-done(((bf16[16,80,512]{2,1,0:T(8,128)(2,1)}), bf16[16,80,512]{2,1,0:T(8,128)(2,1)S(1)}, u32[]{:S(2)}, u32[]{:S(2)}) %all-to-all-start.2) | async-done | bytes 1310752 | tf_op jit(solution)/shard_map/all_to_all | solution.py:28
  142.4 2.6 %collective-permute-done.18.refs_3_ = bf16[144,512]{1,0:T(8,128)(2,1)S(1)} collective-permute-done((bf16[144,512]{1,0:T(8,128)(2,1)S(1)}, bf16[144,512]{1,0:T(8,128)(2,1)S(1)}, u32[]{:S(2)}, u32[]{:S(2)}) %collective-permute-start.18) | collective-permute-done | bytes 147488 | tf_op jit(solution)/shard_map/ppermute | solution.py:33
  150.0 2.3 copy-done
  152.3 4.5 %shard_map.28 = (f32[144,512]{1,0:T(8,128)S(1)}, bf16[160,512]{1,0:T(8,128)(2,1)S(1)}) custom-call(s32[8]{0:T(128)S(1)} %stack.27.pos_ref, f32[144,512]{1,0:T(8,128)S(1)} %pad_maximum_fusion.refs_0_, bf16[16,272,512]{2,1,0:T(8,128)(2,1)S(1)} %bitcast.16, bf16[144,512]{1,0:T(8,128)(2,1)S(1)} %fusion.2.refs_2_, ...), custom_call_target="tpu_custom_call" | custom-call | flops 603979776 | bytes 4194304 | tf_op jit(solution)/shard_map/pallas_call | solution.py:286
  159.5 4.4 %collective-permute-done.25.refs_4_ = bf16[160,512]{1,0:T(8,128)(2,1)S(1)} collective-permute-done((bf16[160,512]{1,0:T(8,128)(2,1)S(1)}, bf16[160,512]{1,0:T(8,128)(2,1)S(1)}, u32[]{:S(2)}, u32[]{:S(2)}) %collective-permute-start.25) | collective-permute-done | bytes 163872 | tf_op jit(solution)/shard_map/ppermute | solution.py:33
  163.9 2.4 %collective-permute-done.26.refs_5_ = bf16[160,512]{1,0:T(8,128)(2,1)S(1)} collective-permute-done((bf16[160,512]{1,0:T(8,128)(2,1)S(1)}, bf16[160,512]{1,0:T(8,128)(2,1)S(1)}, u32[]{:S(2)}, u32[]{:S(2)}) %collective-permute-start.26) | collective-permute-done | bytes 163872 | tf_op jit(solution)/shard_map/ppermute | solution.py:33
  166.3 2.5 %collective-permute-done.27.refs_6_ = bf16[160,512]{1,0:T(8,128)(2,1)S(1)} collective-permute-done((bf16[160,512]{1,0:T(8,128)(2,1)S(1)}, bf16[160,512]{1,0:T(8,128)(2,1)S(1)}, u32[]{:S(2)}, u32[]{:S(2)}) %collective-permute-start.27) | collective-permute-done | bytes 163872 | tf_op jit(solution)/shard_map/ppermute | solution.py:33
  170.3 4.9 %shard_map.29 = (f32[144,768]{1,0:T(8,128)S(1)}, f32[144,512]{1,0:T(8,128)S(1)}, f32[144,512]{1,0:T(8,128)S(1)}, bf16[160,512]{1,0:T(8,128)(2,1)S(1)}) custom-call(s32[8]{0:T(128)S(1)} %stack.27.pos_ref, f32[144,512]{1,0:T(8,128)S(1)} %pad_maximum_fusion.refs_0_, f32[144,512]{1,0:T(8,128)S(1)} %get-tuple-element.27.refs_1_, ...), custom_call_target="tpu_custom_call" | custom-call | flops 603979776 | bytes 4194304 | tf_op jit(solution)/shard_map/pallas_call | solution.py:286
  177.7 4.6 %collective-permute-done.32.refs_7_ = bf16[160,512]{1,0:T(8,128)(2,1)S(1)} collective-permute-done((bf16[160,512]{1,0:T(8,128)(2,1)S(1)}, bf16[160,512]{1,0:T(8,128)(2,1)S(1)}, u32[]{:S(2)}, u32[]{:S(2)}) %collective-permute-start.32) | collective-permute-done | bytes 163872 | tf_op jit(solution)/shard_map/ppermute | solution.py:33
  182.3 2.2 collective-permute-done.33.refs_8_
  184.5 2.5 %collective-permute-done.34.refs_9_ = bf16[160,512]{1,0:T(8,128)(2,1)S(1)} collective-permute-done((bf16[160,512]{1,0:T(8,128)(2,1)S(1)}, bf16[160,512]{1,0:T(8,128)(2,1)S(1)}, u32[]{:S(2)}, u32[]{:S(2)}) %collective-permute-start.34) | collective-permute-done | bytes 163872 | tf_op jit(solution)/shard_map/ppermute | solution.py:33
  188.4 6.0 %shard_map.30 = (f32[144,512]{1,0:T(8,128)S(1)}, f32[144,512]{1,0:T(8,128)S(1)}, f32[144,768]{1,0:T(8,128)S(1)}, f32[8,288]{1,0:T(8,128)S(1)}) custom-call(s32[8]{0:T(128)S(1)} %stack.27.pos_ref, f32[144,512]{1,0:T(8,128)S(1)} %pad_maximum_fusion.refs_0_, f32[144,512]{1,0:T(8,128)S(1)} %get-tuple-element.27.refs_1_, ...), custom_call_target="tpu_custom_call" | custom-call | flops 603979776 | bytes 4194304 | tf_op jit(solution)/shard_map/pallas_call | solution.py:286
  195.0 4.5 %all-to-all-start.3 = ((f32[8,1,288]{2,1,0:T(1,128)}), f32[8,1,288]{2,1,0:T(1,128)S(1)}, u32[]{:S(2)}, u32[]{:S(2)}) async-start(f32[8,1,288]{2,1,0:T(1,128)} %copy.12), calls=%async_computation.3 | async-start | bytes 24576 | tf_op jit(solution)/shard_map/all_to_all | solution.py:28
  199.5 3.3 %all-to-all-done.3 = f32[8,1,288]{2,1,0:T(1,128)S(1)} async-done(((f32[8,1,288]{2,1,0:T(1,128)}), f32[8,1,288]{2,1,0:T(1,128)S(1)}, u32[]{:S(2)}, u32[]{:S(2)}) %all-to-all-start.3) | async-done | bytes 9248 | tf_op jit(solution)/shard_map/all_to_all | solution.py:28
  203.4 3.9 %collective-permute-start.39 = (f32[144,256]{1,0:T(8,128)S(1)}, f32[144,256]{1,0:T(8,128)S(1)}, u32[]{:S(2)}, u32[]{:S(2)}) collective-permute-start(f32[144,256]{1,0:T(8,128)S(1)} %get-tuple-element.41), channel_id=1, source_target_pairs={{0,0},{1,1},{2,16},{3,17},{4,32},{5,33},{6,48},{7,49},{8,64},{9,65... | collective-permute-start | bytes 442376 | tf_op jit(solution)/shard_map/ppermute | solution.py:312
  207.3 2.5 %collective-permute-start.40 = (f32[144,256]{1,0:T(8,128)S(1)}, f32[144,256]{1,0:T(8,128)S(1)}, u32[]{:S(2)}, u32[]{:S(2)}) collective-permute-start(f32[144,256]{1,0:T(8,128)S(1)} %get-tuple-element.42), channel_id=1, source_target_pairs={{0,1},{1,0},{2,17},{3,16},{4,33},{5,32},{6,49},{7,48},{8,65},{9,64... | collective-permute-start | bytes 442376 | tf_op jit(solution)/shard_map/ppermute | solution.py:312
  209.8 13.9 %collective-permute-done.39 = f32[144,256]{1,0:T(8,128)S(1)} collective-permute-done((f32[144,256]{1,0:T(8,128)S(1)}, f32[144,256]{1,0:T(8,128)S(1)}, u32[]{:S(2)}, u32[]{:S(2)}) %collective-permute-start.39) | collective-permute-done | bytes 147488 | tf_op jit(solution)/shard_map/ppermute | solution.py:312
  (95 shorter events, 31.6 us)
Async XLA Ops:
  6.5 143.5 %all-gather.3.cloned.1.call-start = ((), (), s32[]{:S(2)}) async-start(), calls=%async_computation.4 | async-start | bytes 4734976 | tf_op jit(solution)/shard_map/all_gather | solution.py:331
  46.1 13.5 %collective-permute-start = (bf16[1024,256]{1,0:T(8,128)(2,1)S(1)}, bf16[1024,256]{1,0:T(8,128)(2,1)S(1)}, u32[]{:S(2)}, u32[]{:S(2)}) collective-permute-start(bf16[1024,256]{1,0:T(8,128)(2,1)S(1)} %copy-done.2), channel_id=1, source_target_pairs={{0,32},{32,64},{64,96},{96,0},{1,33},{33,65},{65,97},{97,1},{2,34}... | collective-permute-start | bytes 1572872 | tf_op jit(solution)/shard_map/ppermute | solution.py:33
  48.2 14.8 %collective-permute-start.1 = (bf16[1024,256]{1,0:T(8,128)(2,1)S(1)}, bf16[1024,256]{1,0:T(8,128)(2,1)S(1)}, u32[]{:S(2)}, u32[]{:S(2)}) collective-permute-start(bf16[1024,256]{1,0:T(8,128)(2,1)S(1)} %copy-done.2), channel_id=1, source_target_pairs={{0,96},{32,0},{64,32},{96,64},{1,97},{33,1},{65,33},{97,65},{2,98}... | collective-permute-start | bytes 1572872 | tf_op jit(solution)/shard_map/ppermute | solution.py:33
  48.2 19.8 %collective-permute-start.4 = (bf16[1024,256]{1,0:T(8,128)(2,1)S(1)}, bf16[1024,256]{1,0:T(8,128)(2,1)S(1)}, u32[]{:S(2)}, u32[]{:S(2)}) collective-permute-start(bf16[1024,256]{1,0:T(8,128)(2,1)S(1)} %copy-done.2), channel_id=1, source_target_pairs={{0,16},{16,0},{1,17},{17,1},{2,18},{18,2},{3,19},{19,3},{4,20},{20... | collective-permute-start | bytes 1572872 | tf_op jit(solution)/shard_map/ppermute | solution.py:33
  59.6 7.9 %collective-permute-start.2 = (bf16[512,256]{1,0:T(8,128)(2,1)S(1)}, bf16[512,256]{1,0:T(8,128)(2,1)S(1)}, u32[]{:S(2)}, u32[]{:S(2)}) collective-permute-start(bf16[512,256]{1,0:T(8,128)(2,1)S(1)} %slice.44), channel_id=1, source_target_pairs={{0,32},{32,64},{64,96},{96,0},{1,33},{33,65},{65,97},{97,1},{2,34}... | collective-permute-start | bytes 786440 | tf_op jit(solution)/shard_map/ppermute | solution.py:33
  63.0 8.7 %collective-permute-start.3 = (bf16[512,256]{1,0:T(8,128)(2,1)S(1)}, bf16[512,256]{1,0:T(8,128)(2,1)S(1)}, u32[]{:S(2)}, u32[]{:S(2)}) collective-permute-start(bf16[512,256]{1,0:T(8,128)(2,1)S(1)} %slice.45), channel_id=1, source_target_pairs={{0,96},{32,0},{64,32},{96,64},{1,97},{33,1},{65,33},{97,65},{2,98}... | collective-permute-start | bytes 786440 | tf_op jit(solution)/shard_map/ppermute | solution.py:33
  67.5 5.8 %collective-permute-start.5 = (bf16[1024,256]{1,0:T(8,128)(2,1)S(1)}, bf16[1024,256]{1,0:T(8,128)(2,1)S(1)}, u32[]{:S(2)}, u32[]{:S(2)}) collective-permute-start(bf16[1024,256]{1,0:T(8,128)(2,1)S(1)} %collective-permute-done.refs_1_), channel_id=1, source_target_pairs={{0,16},{16,0},{1,17},{17,1},{2,18},{18,2},{3,19},{19,3},{4,20},{20... | collective-permute-start | bytes 1572872 | tf_op jit(solution)/shard_map/ppermute | solution.py:33
  68.0 5.3 %collective-permute-start.6 = (bf16[1024,256]{1,0:T(8,128)(2,1)S(1)}, bf16[1024,256]{1,0:T(8,128)(2,1)S(1)}, u32[]{:S(2)}, u32[]{:S(2)}) collective-permute-start(bf16[1024,256]{1,0:T(8,128)(2,1)S(1)} %collective-permute-done.1.refs_2_), channel_id=1, source_target_pairs={{0,16},{16,0},{1,17},{17,1},{2,18},{18,2},{3,19},{19,3},{4,20},{20... | collective-permute-start | bytes 1572872 | tf_op jit(solution)/shard_map/ppermute | solution.py:33
  68.0 18.7 %collective-permute-start.9 = (bf16[1280,256]{1,0:T(8,128)(2,1)}, bf16[1280,256]{1,0:T(8,128)(2,1)S(1)}, u32[]{:S(2)}, u32[]{:S(2)}) collective-permute-start(bf16[1280,256]{1,0:T(8,128)(2,1)} %get-tuple-element.26.refs_0_), channel_id=1, source_target_pairs={{0,32},{32,64},{64,96},{96,0},{1,33},{33,65},{65,97},{97,1},{2,34}... | collective-permute-start | bytes 1966088 | tf_op jit(solution)/shard_map/ppermute | solution.py:33
  71.7 18.7 %collective-permute-start.10 = (bf16[1280,256]{1,0:T(8,128)(2,1)}, bf16[1280,256]{1,0:T(8,128)(2,1)S(1)}, u32[]{:S(2)}, u32[]{:S(2)}) collective-permute-start(bf16[1280,256]{1,0:T(8,128)(2,1)} %get-tuple-element.26.refs_0_), channel_id=1, source_target_pairs={{0,96},{32,0},{64,32},{96,64},{1,97},{33,1},{65,33},{97,65},{2,98}... | collective-permute-start | bytes 1966088 | tf_op jit(solution)/shard_map/ppermute | solution.py:33
  78.3 35.8 %all-to-all-start.1 = ((bf16[16,64,512]{2,1,0:T(8,128)(2,1)}), bf16[16,64,512]{2,1,0:T(8,128)(2,1)}, u32[]{:S(2)}, u32[]{:S(2)}) async-start(bf16[16,64,512]{2,1,0:T(8,128)(2,1)} %bitcast.8), calls=%async_computation.1 | async-start | bytes 2097152 | tf_op jit(solution)/shard_map/all_to_all | solution.py:28
  86.2 14.6 %collective-permute-start.13 = (bf16[1280,256]{1,0:T(8,128)(2,1)}, bf16[1280,256]{1,0:T(8,128)(2,1)S(1)}, u32[]{:S(2)}, u32[]{:S(2)}) collective-permute-start(bf16[1280,256]{1,0:T(8,128)(2,1)} %get-tuple-element.26.refs_0_), channel_id=1, source_target_pairs={{0,16},{16,0},{1,17},{17,1},{2,18},{18,2},{3,19},{19,3},{4,20},{20... | collective-permute-start | bytes 1966088 | tf_op jit(solution)/shard_map/ppermute | solution.py:33
  86.7 10.5 %collective-permute-start.11 = (bf16[640,256]{1,0:T(8,128)(2,1)S(1)}, bf16[640,256]{1,0:T(8,128)(2,1)S(1)}, u32[]{:S(2)}, u32[]{:S(2)}) collective-permute-start(bf16[640,256]{1,0:T(8,128)(2,1)S(1)} %slice.46), channel_id=1, source_target_pairs={{0,32},{32,64},{64,96},{96,0},{1,33},{33,65},{65,97},{97,1},{2,34}... | collective-permute-start | bytes 983048 | tf_op jit(solution)/shard_map/ppermute | solution.py:33
  90.4 10.4 %collective-permute-start.12 = (bf16[640,256]{1,0:T(8,128)(2,1)S(1)}, bf16[640,256]{1,0:T(8,128)(2,1)S(1)}, u32[]{:S(2)}, u32[]{:S(2)}) collective-permute-start(bf16[640,256]{1,0:T(8,128)(2,1)S(1)} %slice.47), channel_id=1, source_target_pairs={{0,96},{32,0},{64,32},{96,64},{1,97},{33,1},{65,33},{97,65},{2,98}... | collective-permute-start | bytes 983048 | tf_op jit(solution)/shard_map/ppermute | solution.py:33
  90.5 11.9 %collective-permute-start.14 = (bf16[1280,256]{1,0:T(8,128)(2,1)S(1)}, bf16[1280,256]{1,0:T(8,128)(2,1)S(1)}, u32[]{:S(2)}, u32[]{:S(2)}) collective-permute-start(bf16[1280,256]{1,0:T(8,128)(2,1)S(1)} %collective-permute-done.9.refs_1_), channel_id=1, source_target_pairs={{0,16},{16,0},{1,17},{17,1},{2,18},{18,2},{3,19},{19,3},{4,20},{20... | collective-permute-start | bytes 1966088 | tf_op jit(solution)/shard_map/ppermute | solution.py:33
  90.6 11.8 %collective-permute-start.15 = (bf16[1280,256]{1,0:T(8,128)(2,1)S(1)}, bf16[1280,256]{1,0:T(8,128)(2,1)S(1)}, u32[]{:S(2)}, u32[]{:S(2)}) collective-permute-start(bf16[1280,256]{1,0:T(8,128)(2,1)S(1)} %collective-permute-done.10.refs_2_), channel_id=1, source_target_pairs={{0,16},{16,0},{1,17},{17,1},{2,18},{18,2},{3,19},{19,3},{4,20},{20... | collective-permute-start | bytes 1966088 | tf_op jit(solution)/shard_map/ppermute | solution.py:33
  114.1 25.1 %all-to-all-start.2 = ((bf16[16,80,512]{2,1,0:T(8,128)(2,1)}), bf16[16,80,512]{2,1,0:T(8,128)(2,1)S(1)}, u32[]{:S(2)}, u32[]{:S(2)}) async-start(bf16[16,80,512]{2,1,0:T(8,128)(2,1)} %bitcast.9), calls=%async_computation.2 | async-start | bytes 2621440 | tf_op jit(solution)/shard_map/all_to_all | solution.py:28
  139.4 5.6 %collective-permute-start.18 = (bf16[144,512]{1,0:T(8,128)(2,1)S(1)}, bf16[144,512]{1,0:T(8,128)(2,1)S(1)}, u32[]{:S(2)}, u32[]{:S(2)}) collective-permute-start(bf16[144,512]{1,0:T(8,128)(2,1)S(1)} %fusion.2.refs_2_), channel_id=1, source_target_pairs={{0,32},{32,64},{64,96},{96,0},{1,33},{33,65},{65,97},{97,1},{2,34}... | collective-permute-start | bytes 442376 | tf_op jit(solution)/shard_map/ppermute | solution.py:33
  140.1 7.0 %collective-permute-start.19 = (bf16[144,512]{1,0:T(8,128)(2,1)S(1)}, bf16[144,512]{1,0:T(8,128)(2,1)S(1)}, u32[]{:S(2)}, u32[]{:S(2)}) collective-permute-start(bf16[144,512]{1,0:T(8,128)(2,1)S(1)} %fusion.2.refs_2_), channel_id=1, source_target_pairs={{0,64},{32,96},{64,0},{96,32},{1,65},{33,97},{65,1},{97,33},{2,66}... | collective-permute-start | bytes 442376 | tf_op jit(solution)/shard_map/ppermute | solution.py:33
  141.1 7.5 %collective-permute-start.20 = (bf16[144,512]{1,0:T(8,128)(2,1)S(1)}, bf16[144,512]{1,0:T(8,128)(2,1)S(1)}, u32[]{:S(2)}, u32[]{:S(2)}) collective-permute-start(bf16[144,512]{1,0:T(8,128)(2,1)S(1)} %fusion.2.refs_2_), channel_id=1, source_target_pairs={{0,96},{32,0},{64,32},{96,64},{1,97},{33,1},{65,33},{97,65},{2,98}... | collective-permute-start | bytes 442376 | tf_op jit(solution)/shard_map/ppermute | solution.py:33
  142.4 6.2 %collective-permute-start.21 = (bf16[144,512]{1,0:T(8,128)(2,1)S(1)}, bf16[144,512]{1,0:T(8,128)(2,1)S(1)}, u32[]{:S(2)}, u32[]{:S(2)}) collective-permute-start(bf16[144,512]{1,0:T(8,128)(2,1)S(1)} %fusion.2.refs_2_), channel_id=1, source_target_pairs={{0,16},{16,0},{1,17},{17,1},{2,18},{18,2},{3,19},{19,3},{4,20},{20... | collective-permute-start | bytes 442376 | tf_op jit(solution)/shard_map/ppermute | solution.py:33
  156.8 7.1 %collective-permute-start.25 = (bf16[160,512]{1,0:T(8,128)(2,1)S(1)}, bf16[160,512]{1,0:T(8,128)(2,1)S(1)}, u32[]{:S(2)}, u32[]{:S(2)}) collective-permute-start(bf16[160,512]{1,0:T(8,128)(2,1)S(1)} %get-tuple-element.28.refs_3_), channel_id=1, source_target_pairs={{0,32},{32,64},{64,96},{96,0},{1,33},{33,65},{65,97},{97,1},{2,34}... | collective-permute-start | bytes 491528 | tf_op jit(solution)/shard_map/ppermute | solution.py:33
  157.7 8.6 %collective-permute-start.26 = (bf16[160,512]{1,0:T(8,128)(2,1)S(1)}, bf16[160,512]{1,0:T(8,128)(2,1)S(1)}, u32[]{:S(2)}, u32[]{:S(2)}) collective-permute-start(bf16[160,512]{1,0:T(8,128)(2,1)S(1)} %get-tuple-element.28.refs_3_), channel_id=1, source_target_pairs={{0,64},{32,96},{64,0},{96,32},{1,65},{33,97},{65,1},{97,33},{2,66}... | collective-permute-start | bytes 491528 | tf_op jit(solution)/shard_map/ppermute | solution.py:33
  158.8 10.1 %collective-permute-start.27 = (bf16[160,512]{1,0:T(8,128)(2,1)S(1)}, bf16[160,512]{1,0:T(8,128)(2,1)S(1)}, u32[]{:S(2)}, u32[]{:S(2)}) collective-permute-start(bf16[160,512]{1,0:T(8,128)(2,1)S(1)} %get-tuple-element.28.refs_3_), channel_id=1, source_target_pairs={{0,96},{32,0},{64,32},{96,64},{1,97},{33,1},{65,33},{97,65},{2,98}... | collective-permute-start | bytes 491528 | tf_op jit(solution)/shard_map/ppermute | solution.py:33
  159.5 9.4 %collective-permute-start.28 = (bf16[160,512]{1,0:T(8,128)(2,1)S(1)}, bf16[160,512]{1,0:T(8,128)(2,1)S(1)}, u32[]{:S(2)}, u32[]{:S(2)}) collective-permute-start(bf16[160,512]{1,0:T(8,128)(2,1)S(1)} %get-tuple-element.28.refs_3_), channel_id=1, source_target_pairs={{0,16},{16,0},{1,17},{17,1},{2,18},{18,2},{3,19},{19,3},{4,20},{20... | collective-permute-start | bytes 491528 | tf_op jit(solution)/shard_map/ppermute | solution.py:33
  175.1 7.1 %collective-permute-start.32 = (bf16[160,512]{1,0:T(8,128)(2,1)S(1)}, bf16[160,512]{1,0:T(8,128)(2,1)S(1)}, u32[]{:S(2)}, u32[]{:S(2)}) collective-permute-start(bf16[160,512]{1,0:T(8,128)(2,1)S(1)} %get-tuple-element.32.refs_6_), channel_id=1, source_target_pairs={{0,32},{32,64},{64,96},{96,0},{1,33},{33,65},{65,97},{97,1},{2,34}... | collective-permute-start | bytes 491528 | tf_op jit(solution)/shard_map/ppermute | solution.py:33
  175.8 8.6 %collective-permute-start.33 = (bf16[160,512]{1,0:T(8,128)(2,1)S(1)}, bf16[160,512]{1,0:T(8,128)(2,1)S(1)}, u32[]{:S(2)}, u32[]{:S(2)}) collective-permute-start(bf16[160,512]{1,0:T(8,128)(2,1)S(1)} %get-tuple-element.32.refs_6_), channel_id=1, source_target_pairs={{0,64},{32,96},{64,0},{96,32},{1,65},{33,97},{65,1},{97,33},{2,66}... | collective-permute-start | bytes 491528 | tf_op jit(solution)/shard_map/ppermute | solution.py:33
  176.9 10.1 %collective-permute-start.34 = (bf16[160,512]{1,0:T(8,128)(2,1)S(1)}, bf16[160,512]{1,0:T(8,128)(2,1)S(1)}, u32[]{:S(2)}, u32[]{:S(2)}) collective-permute-start(bf16[160,512]{1,0:T(8,128)(2,1)S(1)} %get-tuple-element.32.refs_6_), channel_id=1, source_target_pairs={{0,96},{32,0},{64,32},{96,64},{1,97},{33,1},{65,33},{97,65},{2,98}... | collective-permute-start | bytes 491528 | tf_op jit(solution)/shard_map/ppermute | solution.py:33
  177.7 9.3 %collective-permute-start.35 = (bf16[160,512]{1,0:T(8,128)(2,1)S(1)}, bf16[160,512]{1,0:T(8,128)(2,1)S(1)}, u32[]{:S(2)}, u32[]{:S(2)}) collective-permute-start(bf16[160,512]{1,0:T(8,128)(2,1)S(1)} %get-tuple-element.32.refs_6_), channel_id=1, source_target_pairs={{0,16},{16,0},{1,17},{17,1},{2,18},{18,2},{3,19},{19,3},{4,20},{20... | collective-permute-start | bytes 491528 | tf_op jit(solution)/shard_map/ppermute | solution.py:33
  195.0 7.8 %all-to-all-start.3 = ((f32[8,1,288]{2,1,0:T(1,128)}), f32[8,1,288]{2,1,0:T(1,128)S(1)}, u32[]{:S(2)}, u32[]{:S(2)}) async-start(f32[8,1,288]{2,1,0:T(1,128)} %copy.12), calls=%async_computation.3 | async-start | bytes 24576 | tf_op jit(solution)/shard_map/all_to_all | solution.py:28
  203.4 20.3 %collective-permute-start.39 = (f32[144,256]{1,0:T(8,128)S(1)}, f32[144,256]{1,0:T(8,128)S(1)}, u32[]{:S(2)}, u32[]{:S(2)}) collective-permute-start(f32[144,256]{1,0:T(8,128)S(1)} %get-tuple-element.41), channel_id=1, source_target_pairs={{0,0},{1,1},{2,16},{3,17},{4,32},{5,33},{6,48},{7,49},{8,64},{9,65... | collective-permute-start | bytes 442376 | tf_op jit(solution)/shard_map/ppermute | solution.py:312
  207.3 16.4 %collective-permute-start.40 = (f32[144,256]{1,0:T(8,128)S(1)}, f32[144,256]{1,0:T(8,128)S(1)}, u32[]{:S(2)}, u32[]{:S(2)}) collective-permute-start(f32[144,256]{1,0:T(8,128)S(1)} %get-tuple-element.42), channel_id=1, source_target_pairs={{0,1},{1,0},{2,17},{3,16},{4,33},{5,32},{6,49},{7,48},{8,65},{9,64... | collective-permute-start | bytes 442376 | tf_op jit(solution)/shard_map/ppermute | solution.py:312
  (17 other events, 42.3 us)
Sparse Core Ops, SparseCore 0:
  46.2 65.5 all-gather.2
where the time goes:
time: 232 us; the launch traced here: 231 us
  waiting for transfers between devices  102 us (44%)
  starting transfers between devices  45.3 us (20%)
  blocking collectives  31 us (13%)
  Pallas kernels  30.4 us (13%)
  between operations  13.6 us (6%)
  local copies, waits for them, and re-layouts  6.57 us (3%)
  other arithmetic  2.7 us (1%)
    ppermute x39, waiting for transfers between devices, turn(): lax.ppermute(block, axis, [(i, (i + step) % size) for i in range(size)])  57.8 us
    all_to_all x1, blocking collectives, exchange(): return lax.all_to_all(parts, axis, split_axis=0, concat_axis=0, tiled=True)  31 us
    all_to_all x3, waiting for transfers between devices, exchange(): return lax.all_to_all(parts, axis, split_axis=0, concat_axis=0, tiled=True)  29.9 us
    ppermute x39, starting transfers between devices, turn(): lax.ppermute(block, axis, [(i, (i + step) % size) for i in range(size)])  22.8 us
    all_to_all x3, starting transfers between devices, exchange(): return lax.all_to_all(parts, axis, split_axis=0, concat_axis=0, tiled=True)  16.1 us
    pallas_call x3, Pallas kernels, run(): pl.pallas_call(kernel, in_specs=[SMEM] + [VMEM] * len(owns) + [HBM] * (1...  15.3 us
    ppermute x2, waiting for transfers between devices, to_output(): came.append(lax.ppermute(sent, ALL, pairs))  13.9 us
    pallas_call x2, Pallas kernels, right_side_part(): pl.pallas_call(right_side_kernel, in_specs=[SMEM, VMEM] + [VMEM] * len(bl...  8.96 us
  transfers between devices with their start and end apart: 45, of which 23 were waited for; matrix products, arithmetic and copies ran while one was open for 1% of the time, Pallas kernels for 4%

commit v1 on v0

--- a/solution.py
+++ b/solution.py
@@ -91,13 +91,12 @@
         in_specs=[SMEM, pl.BlockSpec((ROWS, 2 * CHUNK), lambda i: (0, i))],
         out_specs=pl.BlockSpec((2, FULL, CHUNK), lambda i: (i, 0, 0)),
         out_shape=jax.ShapeDtypeStruct((chunks, FULL, CHUNK), BF16),
-        compiler_params=LIMIT,
         cost_estimate=cost(10**8, gram.size * 6),
         name="spread_grams",
     )(pos, gram)
 
 
-def sum_kernel(pos_ref, blocks_ref, out_ref):
+def sum_kernel(pos_ref, blocks_ref, *out_refs):
     total = jnp.sum(blocks_ref[...].astype(F32), axis=0)
     block, rest = total[:ROWS], total[ROWS : ROWS + 1]
     row = lax.broadcasted_iota(jnp.int32, block.shape, 0) + pos_ref[3] * ROWS
@@ -107,28 +106,44 @@
     kept = low.astype(F32)
     diag = jnp.sum(jnp.where(on, kept, 0.0), axis=0, keepdims=True)
     rest = rest + jnp.sum(jnp.where(on, block - kept, 0.0), axis=0, keepdims=True)
-    out_ref[:ROWS] = low
-    out_ref[ROWS:] = spare_rows(diag, rest)
+    spare = spare_rows(diag, rest)
+    half = CHUNK // 2
+    for h, out_ref in enumerate(out_refs):
+        out_ref[:ROWS] = low[:, h * half : (h + 1) * half]
+        out_ref[ROWS:] = spare[:, h * half : (h + 1) * half]
 
 
 def sum_grams(pos, blocks):
+    half = jax.ShapeDtypeStruct((FULL, CHUNK // 2), BF16)
     return pl.pallas_call(
         sum_kernel,
         in_specs=[SMEM, VMEM],
-        out_specs=VMEM,
-        out_shape=jax.ShapeDtypeStruct((FULL, CHUNK), BF16),
+        out_specs=[VMEM, VMEM],
+        out_shape=[half, half],
         compiler_params=LIMIT,
         cost_estimate=cost(10**8, blocks.size * 2),
         name="sum_grams",
     )(pos, blocks)
 
 
+def gather_line(half, axis):
+    return jnp.stack([half] + [turn(half, axis, step) for step in (1, 2, 3)])
+
+
+def gather_plane(lines):
+    out = []
+    for line, axis in zip(lines, ("z", "x")):
+        out += [line] + [turn(line, axis, step) for step in (1, 2, 3)]
+    return out
+
+
 def gather_weights(piece):
     middle = piece.shape[0] // 2
     up, down = turn(piece, "y", 1), turn(piece, "y", 3)
     far = [turn(up[:middle], "y", 1), turn(down[middle:], "y", 3)]
-    mine = [piece, up, down] + far
-    return mine + [turn(b, "core", 1) for b in mine]
+    others = [turn(b, "core", 1) for b in (piece, up, down)]
+    others += [turn(b, "core", 1) for b in far]
+    return [piece, up, down] + far + others
 
 
 def right_side_kernel(pos_ref, g_ref, *refs):
@@ -168,33 +183,40 @@
     return mine + [turn(b, "core", 1) for b in mine]
 
 
-def fetch(pos_ref, gram_hbm, parts, gram_ref, all_ref, sems):
+def fetch(pos_ref, parts, all_ref, sems):
     y, core = pos_ref[0], pos_ref[1]
     copies = []
     for i, part in enumerate(parts):
         at = lax.rem(y + 4 - i % 4, 4) * 2 + (core if i < 4 else 1 - core)
         copies.append(pltpu.make_async_copy(part, all_ref.at[at], sems.at[i]))
-    grams = []
-    for i in range(4):
-        some = pl.ds(4 * i, 4)
-        grams.append(pltpu.make_async_copy(gram_hbm.at[some], gram_ref.at[some], sems.at[8 + i]))
-    for copy in copies + grams:
+    for copy in copies:
         copy.start()
     for copy in copies:
         copy.wait()
-    return 2 * y + core, grams
-
-
-def product(gram_ref, all_ref, at, grams, own):
-    total = jnp.zeros(own.shape, F32)
-    spare = jnp.zeros((8, CHUNK), F32)
-    for s in range(16):
-        if s % 4 == 0:
-            grams[s // 4].wait()
-        h = s % 2
-        total += dot(all_ref[s // 2, :COLS, h * ROWS : (h + 1) * ROWS], gram_ref[s, :ROWS])
-        spare += gram_ref[s, ROWS:].astype(F32)[:8]
-    return total + spare[0:1] * (own - all_ref[at, :COLS].astype(F32)) + spare[1:2] * own
+    return 2 * y + core
+
+
+def product(pos_ref, gram_refs, all_ref, at, own):
+    z, x = pos_ref[5], pos_ref[6]
+    sums = []
+    spare = []
+    for half in range(2):
+        total = jnp.zeros((own.shape[0], CHUNK // 2), F32)
+        extra = jnp.zeros((8, CHUNK // 2), F32)
+        for a in range(4):
+            for b in range(4):
+                k, j = (a, b) if half == 0 else (b, a)
+                j = lax.rem(x + 4 - j, 4)
+                chunk = 2 * lax.rem(z + 4 - k, 4) + lax.div(j, 2)
+                lanes = pl.ds(pl.multiple_of(lax.rem(j, 2) * ROWS, ROWS), ROWS)
+                ref = gram_refs[4 * half + a]
+                total += dot(all_ref[chunk, : own.shape[0], lanes], ref[b, :ROWS])
+                extra += ref[b, ROWS:].astype(F32)[:8]
+        sums.append(total)
+        spare.append(extra)
+    total = jnp.concatenate(sums, axis=1)
+    spare = jnp.concatenate(spare, axis=1)
+    return total + spare[0:1] * (own - all_ref[at, : own.shape[0]].astype(F32)) + spare[1:2] * own
 
 
 def own_sum(a, b):
@@ -256,7 +278,7 @@
 
 def third_kernel(times, sums, own_refs, outs):
     r0, w0, z0, r1, w1 = (ref[...] for ref in own_refs)
-    x_ref, r2_ref, p_ref, sums_ref = outs
+    last_ref, sums_ref = outs
     norm0, step0 = z0[:, CHUNK : CHUNK + 1], z0[:, CHUNK + 128 : CHUNK + 129]
     z0 = z0[:, :CHUNK]
     norm1, curve1 = sums()
@@ -264,38 +286,39 @@
     step1 = norm1 / (curve1 - beta1 * norm1 / step0)
     p1 = r1 + beta1 * r0
     r2 = r1 - step1 * (w1 + beta1 * w0)
-    x_ref[...] = step0 * r0 + step1 * p1
-    r2_ref[...] = r2
-    p_ref[:, :CHUNK] = p1
-    p_ref[:, CHUNK : CHUNK + 128] = wide(norm1)
-    p_ref[:, CHUNK + 128 :] = wide(step1)
+    last_ref[:, :CHUNK] = step0 * r0 + step1 * p1
+    last_ref[:, CHUNK : 2 * CHUNK] = r2
+    last_ref[:, 2 * CHUNK : 3 * CHUNK] = p1
+    last_ref[:, 3 * CHUNK : 3 * CHUNK + 128] = wide(norm1)
+    last_ref[:, 3 * CHUNK + 128 :] = wide(step1)
     norm2 = own_sum(r2, r2)
     w2 = w1 - step1 * (times(w1) + beta1 * z0)
-    sums_ref[...] = jnp.concatenate([norm2, own_sum(r2, w2)], axis=1)
-
-
-def run(body, outs, gram_sum, parts, pos, *owns):
+    sums_ref[:, 0, :] = jnp.concatenate([norm2, own_sum(r2, w2)], axis=1)
+
+
+def run(body, outs, grams, parts, pos, *owns):
     rows = parts[0].shape[0]
 
     def kernel(pos_ref, *refs):
-        own_refs, gram_hbm, part_refs = refs[: len(owns)], refs[len(owns)], refs[len(owns) + 1 : len(owns) + 9]
-        out_refs, (gram_ref, all_ref, sems) = refs[len(owns) + 9 : -3], refs[-3:]
-        at, grams = fetch(pos_ref, gram_hbm, part_refs, gram_ref, all_ref, sems)
-        body(lambda own: product(gram_ref, all_ref, at, grams, own), lambda: take(all_ref), own_refs, out_refs)
+        groups = []
+        for n in (len(owns), len(grams), len(parts), len(outs)):
+            groups.append(refs[:n])
+            refs = refs[n:]
+        own_refs, gram_refs, part_refs, out_refs = groups
+        all_ref, sems = refs
+        at = fetch(pos_ref, part_refs, all_ref, sems)
+        times = lambda own: product(pos_ref, gram_refs, all_ref, at, own)
+        body(times, lambda: take(all_ref), own_refs, out_refs)
 
     return pl.pallas_call(
         kernel,
-        in_specs=[SMEM] + [VMEM] * len(owns) + [HBM] * (1 + len(parts)),
+        in_specs=[SMEM] + [VMEM] * (len(owns) + len(grams)) + [HBM] * len(parts),
         out_specs=[VMEM] * len(outs),
         out_shape=outs,
-        scratch_shapes=[
-            pltpu.VMEM(gram_sum.shape, BF16),
-            pltpu.VMEM((8, rows, CHUNK), BF16),
-            pltpu.SemaphoreType.DMA((12,)),
-        ],
+        scratch_shapes=[pltpu.VMEM((8, rows, CHUNK), BF16), pltpu.SemaphoreType.DMA((8,))],
         compiler_params=LIMIT,
         cost_estimate=cost(2 * COLS * CHUNK * 4096, 4096 * CHUNK * 2),
-    )(pos, *owns, gram_sum, *parts)
+    )(pos, *owns, *grams, *parts)
 
 
 def to_output(block):
@@ -328,7 +351,7 @@
     grams = exchange(spread, MEMBER)
     late, grams = lax.optimization_barrier((pieces[1], grams))
     late = gather_weights(late)
-    gram_sum = lax.all_gather(sum_grams(pos, grams), SHARD, axis=0)
+    gram_sum = gather_plane([gather_line(half, axis) for half, axis in zip(sum_grams(pos, grams), ("x", "z"))])
     parts = []
     for piece, blocks in zip(PIECES, (early, late)):
         part = right_side_part(pos, grams, blocks)
@@ -339,15 +362,16 @@
     array = jax.ShapeDtypeStruct((COLS, CHUNK), F32)
     more = jax.ShapeDtypeStruct((COLS, CHUNK + 256), F32)
     sent = jax.ShapeDtypeStruct((COLS + 16, CHUNK), BF16)
-    sums = jax.ShapeDtypeStruct((8, 2 * COLS), F32)
+    packed = jax.ShapeDtypeStruct((COLS, 3 * CHUNK + 256), F32)
+    sums = jax.ShapeDtypeStruct((8, 1, 2 * COLS), F32)
     w0, low = run(first_kernel, (array, sent), gram_sum, gather(r0.astype(BF16)), pos, r0)
     outs = (more, array, array, sent)
     z0, r1, w1, low = run(second_kernel, outs, gram_sum, gather(low), pos, r0, w0)
-    outs = (array, array, more, sums)
-    x1, r2, p1, both = run(third_kernel, outs, gram_sum, gather(low), pos, r0, w0, z0, r1, w1)
-    norm1, step1 = p1[:, CHUNK : CHUNK + 1], p1[:, CHUNK + 128 : CHUNK + 129]
-    p1 = p1[:, :CHUNK]
-    both = jnp.sum(exchange(both.reshape(8, 1, 2 * COLS), MEMBER), axis=(0, 1))
+    outs = (packed, sums)
+    last, both = run(third_kernel, outs, gram_sum, gather(low), pos, r0, w0, z0, r1, w1)
+    x1, r2, p1 = (last[:, i * CHUNK : (i + 1) * CHUNK] for i in range(3))
+    norm1, step1 = last[:, 3 * CHUNK : 3 * CHUNK + 1], last[:, 3 * CHUNK + 128 : 3 * CHUNK + 129]
+    both = sum(gather(both))[0, 0]
     norm2, curve2 = both[:COLS, None], both[COLS:, None]
     beta2 = norm2 / norm1
     step2 = norm2 / (curve2 - beta2 * norm2 / step1)

time: 232 us -> 264 us (1.14)
  the two profiles are of different devices: /device:TPU:24 before, /device:TPU:101 now
where the time goes in v1:
time: 264 us; the launch traced here: 263 us
  waiting for transfers between devices  128 us (48%)
  starting transfers between devices  89.3 us (34%)
  Pallas kernels  31.9 us (12%)
  local copies, waits for them, and re-layouts  6.8 us (3%)
  other arithmetic  6.21 us (2%)
    ppermute x58, waiting for transfers between devices, turn(): lax.ppermute(block, axis, [(i, (i + step) % size) for i in range(size)])  110 us
    ppermute x58, starting transfers between devices, turn(): lax.ppermute(block, axis, [(i, (i + step) % size) for i in range(size)])  69 us
    all_to_all x3, starting transfers between devices, exchange(): return lax.all_to_all(parts, axis, split_axis=0, concat_axis=0, tiled=True)  18.3 us
    ppermute x2, waiting for transfers between devices, to_output(): came.append(lax.ppermute(sent, ALL, pairs))  18.2 us
    pallas_call x3, Pallas kernels, run(): pl.pallas_call(kernel, in_specs=[SMEM] + [VMEM] * (len(owns) + len(grams)...  13.6 us
    pallas_call x2, Pallas kernels, right_side_part(): pl.pallas_call(right_side_kernel, in_specs=[SMEM, VMEM] + [VMEM] * len(bl...  10.1 us
  transfers between devices with their start and end apart: 63, of which 22 were waited for; matrix products, arithmetic and copies ran while one was open for 2% of the time, Pallas kernels for 4%

profile of v1, /device:TPU:101, one launch (start us, length us, event | category | flops | bytes accessed | tf_op | source)
XLA Modules:
  0.0 263.0 jit_solution(8728788319173336949)
XLA Ops:
  0.0 2.4 turn_weights.1
  3.0 4.8 %spread_grams.1 = bf16[8,272,512]{2,1,0:T(8,128)(2,1)} custom-call(s32[8]{0:T(128)} %stack.57.pos_ref, f32[256,4096]{1,0:T(8,128)} %bitcast.36), custom_call_target="tpu_custom_call" | custom-call | flops 100000000 | bytes 6291456 | tf_op jit(solution)/shard_map/spread_grams/pallas_call | solution.py:88
  7.8 5.3 %all-to-all-start = ((bf16[8,272,512]{2,1,0:T(8,128)(2,1)}), bf16[8,272,512]{2,1,0:T(8,128)(2,1)S(1)}, u32[]{:S(2)}, u32[]{:S(2)}) async-start(bf16[8,272,512]{2,1,0:T(8,128)(2,1)} %spread_grams.1), calls=%async_computation | async-start | bytes 4456448 | tf_op jit(solution)/shard_map/all_to_all | solution.py:28
  16.4 35.5 %collective-permute-done.refs_1_ = bf16[1024,256]{1,0:T(8,128)(2,1)} collective-permute-done((bf16[1024,256]{1,0:T(8,128)(2,1)S(1)}, bf16[1024,256]{1,0:T(8,128)(2,1)}, u32[]{:S(2)}, u32[]{:S(2)}) %collective-permute-start) | collective-permute-done | bytes 524320 | tf_op jit(solution)/shard_map/ppermute | solution.py:33
  54.0 2.7 %collective-permute-start.3 = (bf16[512,256]{1,0:T(8,128)(2,1)S(1)}, bf16[512,256]{1,0:T(8,128)(2,1)}, u32[]{:S(2)}, u32[]{:S(2)}) collective-permute-start(bf16[512,256]{1,0:T(8,128)(2,1)S(1)} %slice.58), channel_id=1, source_target_pairs={{0,96},{32,0},{64,32},{96,64},{1,97},{33,1},{65,33},{97,65},{2,98}... | collective-permute-start | bytes 786440 | tf_op jit(solution)/shard_map/ppermute | solution.py:33
  56.7 4.7 %collective-permute-done.2.refs_3_ = bf16[512,256]{1,0:T(8,128)(2,1)} collective-permute-done((bf16[512,256]{1,0:T(8,128)(2,1)S(1)}, bf16[512,256]{1,0:T(8,128)(2,1)}, u32[]{:S(2)}, u32[]{:S(2)}) %collective-permute-start.2) | collective-permute-done | bytes 262176 | tf_op jit(solution)/shard_map/ppermute | solution.py:33
  64.4 2.7 %collective-permute-start.10 = (bf16[1280,256]{1,0:T(8,128)(2,1)}, bf16[1280,256]{1,0:T(8,128)(2,1)S(1)}, u32[]{:S(2)}, u32[]{:S(2)}) collective-permute-start(bf16[1280,256]{1,0:T(8,128)(2,1)} %get-tuple-element.26.refs_0_), channel_id=1, source_target_pairs={{0,96},{32,0},{64,32},{96,64},{1,97},{33,1},{65,33},{97,65},{2,98}... | collective-permute-start | bytes 1966088 | tf_op jit(solution)/shard_map/ppermute | solution.py:33
  71.1 5.1 %right_side.2 = bf16[1024,512]{1,0:T(8,128)(2,1)} custom-call(s32[8]{0:T(128)S(1)} %copy-done.1, bf16[8,272,512]{2,1,0:T(8,128)(2,1)S(1)} %all-to-all-done.g_ref.blocks_ref, bf16[1024,256]{1,0:T(8,128)(2,1)S(1)} %copy-done.3, bf16[1024,256]{1,0:T(8,128)(2,1)} %collective-permute-done.refs_1_, bf16[1024,256]{1,0:T(8,128)(2,1)} %collective-permute-done.1.refs_2_, ...), custom_call_target="tpu_custom_call" | custom-call | flops 2147483648 | bytes 7471104 | tf_op jit(solution)/shard_map/right_side/pallas_call | solution.py:170
  76.2 6.4 %all-to-all-start.1 = ((bf16[16,64,512]{2,1,0:T(8,128)(2,1)}), bf16[16,64,512]{2,1,0:T(8,128)(2,1)}, u32[]{:S(2)}, u32[]{:S(2)}) async-start(bf16[16,64,512]{2,1,0:T(8,128)(2,1)} %bitcast.8), calls=%async_computation.1 | async-start | bytes 2097152 | tf_op jit(solution)/shard_map/all_to_all | solution.py:28
  83.6 2.7 %collective-permute-start.12 = (bf16[640,256]{1,0:T(8,128)(2,1)S(1)}, bf16[640,256]{1,0:T(8,128)(2,1)S(1)}, u32[]{:S(2)}, u32[]{:S(2)}) collective-permute-start(bf16[640,256]{1,0:T(8,128)(2,1)S(1)} %slice.60), channel_id=1, source_target_pairs={{0,96},{32,0},{64,32},{96,64},{1,97},{33,1},{65,33},{97,65},{2,98}... | collective-permute-start | bytes 983048 | tf_op jit(solution)/shard_map/ppermute | solution.py:33
  86.9 7.2 %collective-permute-done.11.refs_3_ = bf16[640,256]{1,0:T(8,128)(2,1)S(1)} collective-permute-done((bf16[640,256]{1,0:T(8,128)(2,1)S(1)}, bf16[640,256]{1,0:T(8,128)(2,1)S(1)}, u32[]{:S(2)}, u32[]{:S(2)}) %collective-permute-start.11) | collective-permute-done | bytes 327712 | tf_op jit(solution)/shard_map/ppermute | solution.py:33
  96.6 5.0 %right_side.3 = bf16[1280,512]{1,0:T(8,128)(2,1)} custom-call(s32[8]{0:T(128)S(1)} %copy-done.1, bf16[8,272,512]{2,1,0:T(8,128)(2,1)S(1)} %all-to-all-done.g_ref.blocks_ref, bf16[1280,256]{1,0:T(8,128)(2,1)} %get-tuple-element.26.refs_0_, bf16[1280,256]{1,0:T(8,128)(2,1)S(1)} %collective-permute-done.9.refs_1_, ...), custom_call_target="tpu_custom_call" | custom-call | flops 2684354560 | bytes 8781824 | tf_op jit(solution)/shard_map/right_side/pallas_call | solution.py:170
  101.7 6.7 %all-to-all-start.2 = ((bf16[16,80,512]{2,1,0:T(8,128)(2,1)}), bf16[16,80,512]{2,1,0:T(8,128)(2,1)}, u32[]{:S(2)}, u32[]{:S(2)}) async-start(bf16[16,80,512]{2,1,0:T(8,128)(2,1)} %bitcast.9), calls=%async_computation.2 | async-start | bytes 2621440 | tf_op jit(solution)/shard_map/all_to_all | solution.py:28
  111.7 19.7 %collective-permute-done.18 = bf16[272,256]{1,0:T(8,128)(2,1)S(1)} collective-permute-done((bf16[272,256]{1,0:T(8,128)(2,1)S(1)}, bf16[272,256]{1,0:T(8,128)(2,1)S(1)}, u32[]{:S(2)}, u32[]{:S(2)}) %collective-permute-start.18) | collective-permute-done | bytes 139296 | tf_op jit(solution)/shard_map/ppermute | solution.py:33
  135.2 2.3 collective-permute-start.22
  137.5 10.8 %collective-permute-done.24 = bf16[272,256]{1,0:T(8,128)(2,1)S(1)} collective-permute-done((bf16[272,256]{1,0:T(8,128)(2,1)S(1)}, bf16[272,256]{1,0:T(8,128)(2,1)S(1)}, u32[]{:S(2)}, u32[]{:S(2)}) %collective-permute-start.24) | collective-permute-done | bytes 139296 | tf_op jit(solution)/shard_map/ppermute | solution.py:33
  154.3 12.2 %collective-permute-done.23.refs_4_.refs_5_.refs_8_ = bf16[4,272,256]{2,1,0:T(8,128)(2,1)S(1)} collective-permute-done((bf16[4,272,256]{2,1,0:T(8,128)(2,1)S(1)}, bf16[4,272,256]{2,1,0:T(8,128)(2,1)S(1)}, u32[]{:S(2)}, u32[]{:S(2)}) %collective-permute-start.23) | collective-permute-done | bytes 557088 | tf_op jit(solution)/shard_map/ppermute | solution.py:33
  168.8 15.2 %collective-permute-start.33 = (bf16[144,512]{1,0:T(8,128)(2,1)S(1)}, bf16[144,512]{1,0:T(8,128)(2,1)S(1)}, u32[]{:S(2)}, u32[]{:S(2)}) collective-permute-start(bf16[144,512]{1,0:T(8,128)(2,1)S(1)} %fusion.2.refs_9_), channel_id=1, source_target_pairs={{0,16},{16,0},{1,17},{17,1},{2,18},{18,2},{3,19},{19,3},{4,20},{20... | collective-permute-start | bytes 442376 | tf_op jit(solution)/shard_map/ppermute | solution.py:33
  184.5 2.2 collective-permute-start.36
  187.7 4.2 %shard_map.28 = (f32[144,512]{1,0:T(8,128)S(1)}, bf16[160,512]{1,0:T(8,128)(2,1)S(1)}) custom-call(s32[8]{0:T(128)S(1)} %copy-done.1, f32[144,512]{1,0:T(8,128)S(1)} %pad_maximum_fusion.2.refs_0_, bf16[4,272,256]{2,1,0:T(8,128)(2,1)S(1)} %pad_maximum_fusion.refs_1_.refs_2_.refs_5_, bf16[4,272,256]{2,1,0:T(8,128)(2,1)S(1)} %collective-permute-done.21.refs_2_.refs_3_.refs_6_, ...), custom_call_target="tpu_custom_call" | custom-call | flops 603979776 | bytes 4194304 | tf_op jit(solution)/shard_map/pallas_call | solution.py:313
  192.0 4.6 %collective-permute-start.38 = (bf16[160,512]{1,0:T(8,128)(2,1)S(1)}, bf16[160,512]{1,0:T(8,128)(2,1)S(1)}, u32[]{:S(2)}, u32[]{:S(2)}) collective-permute-start(bf16[160,512]{1,0:T(8,128)(2,1)S(1)} %get-tuple-element.30.refs_10_), channel_id=1, source_target_pairs={{0,64},{32,96},{64,0},{96,32},{1,65},{33,97},{65,1},{97,33},{2,66}... | collective-permute-start | bytes 491528 | tf_op jit(solution)/shard_map/ppermute | solution.py:33
  197.5 2.1 collective-permute-done.37.refs_11_
  200.6 3.5 %collective-permute-done.38.refs_12_ = bf16[160,512]{1,0:T(8,128)(2,1)S(1)} collective-permute-done((bf16[160,512]{1,0:T(8,128)(2,1)S(1)}, bf16[160,512]{1,0:T(8,128)(2,1)S(1)}, u32[]{:S(2)}, u32[]{:S(2)}) %collective-permute-start.38) | collective-permute-done | bytes 163872 | tf_op jit(solution)/shard_map/ppermute | solution.py:33
  206.7 4.5 %shard_map.29 = (f32[144,768]{1,0:T(8,128)S(1)}, f32[144,512]{1,0:T(8,128)S(1)}, f32[144,512]{1,0:T(8,128)S(1)}, bf16[160,512]{1,0:T(8,128)(2,1)S(1)}) custom-call(s32[8]{0:T(128)S(1)} %copy-done.1, f32[144,512]{1,0:T(8,128)S(1)} %pad_maximum_fusion.2.refs_0_, f32[144,512]{1,0:T(8,128)S(1)} %get-tuple-element.29.refs_1_, ...), custom_call_target="tpu_custom_call" | custom-call | flops 603979776 | bytes 4194304 | tf_op jit(solution)/shard_map/pallas_call | solution.py:313
  211.2 2.7 %collective-permute-start.45 = (bf16[160,512]{1,0:T(8,128)(2,1)S(1)}, bf16[160,512]{1,0:T(8,128)(2,1)S(1)}, u32[]{:S(2)}, u32[]{:S(2)}) collective-permute-start(bf16[160,512]{1,0:T(8,128)(2,1)S(1)} %get-tuple-element.34.refs_13_), channel_id=1, source_target_pairs={{0,64},{32,96},{64,0},{96,32},{1,65},{33,97},{65,1},{97,33},{2,66}... | collective-permute-start | bytes 491528 | tf_op jit(solution)/shard_map/ppermute | solution.py:33
  214.8 3.2 %collective-permute-done.44.refs_14_ = bf16[160,512]{1,0:T(8,128)(2,1)S(1)} collective-permute-done((bf16[160,512]{1,0:T(8,128)(2,1)S(1)}, bf16[160,512]{1,0:T(8,128)(2,1)S(1)}, u32[]{:S(2)}, u32[]{:S(2)}) %collective-permute-start.44) | collective-permute-done | bytes 163872 | tf_op jit(solution)/shard_map/ppermute | solution.py:33
  224.2 4.9 %shard_map.30 = (f32[144,1792]{1,0:T(8,128)S(1)}, f32[8,1,288]{2,1,0:T(1,128)S(1)}) custom-call(s32[8]{0:T(128)S(1)} %copy-done.1, f32[144,512]{1,0:T(8,128)S(1)} %pad_maximum_fusion.2.refs_0_, f32[144,512]{1,0:T(8,128)S(1)} %get-tuple-element.29.refs_1_, f32[144,768]{1,0:T(8,128)S(1)} %get-tuple-element.31.refs_2_, ...), custom_call_target="tpu_custom_call" | custom-call | flops 603979776 | bytes 4194304 | tf_op jit(solution)/shard_map/pallas_call | solution.py:313
  230.1 2.1 collective-permute-start.53
  234.2 2.0 collective-permute-done.52
  236.2 1.8 collective-permute-start.56
  241.9 1.9 collective-permute-start.58
  244.0 18.2 %collective-permute-done.58 = f32[144,256]{1,0:T(8,128)S(1)} collective-permute-done((f32[144,256]{1,0:T(8,128)S(1)}, f32[144,256]{1,0:T(8,128)S(1)}, u32[]{:S(2)}, u32[]{:S(2)}) %collective-permute-start.58) | collective-permute-done | bytes 147488 | tf_op jit(solution)/shard_map/ppermute | solution.py:335
  (134 shorter events, 53.4 us)
Async XLA Ops:
  7.8 55.7 %all-to-all-start = ((bf16[8,272,512]{2,1,0:T(8,128)(2,1)}), bf16[8,272,512]{2,1,0:T(8,128)(2,1)S(1)}, u32[]{:S(2)}, u32[]{:S(2)}) async-start(bf16[8,272,512]{2,1,0:T(8,128)(2,1)} %spread_grams.1), calls=%async_computation | async-start | bytes 4456448 | tf_op jit(solution)/shard_map/all_to_all | solution.py:28
  13.1 38.8 %collective-permute-start = (bf16[1024,256]{1,0:T(8,128)(2,1)S(1)}, bf16[1024,256]{1,0:T(8,128)(2,1)}, u32[]{:S(2)}, u32[]{:S(2)}) collective-permute-start(bf16[1024,256]{1,0:T(8,128)(2,1)S(1)} %copy-done.2), channel_id=1, source_target_pairs={{0,32},{32,64},{64,96},{96,0},{1,33},{33,65},{65,97},{97,1},{2,34}... | collective-permute-start | bytes 1572872 | tf_op jit(solution)/shard_map/ppermute | solution.py:33
  14.5 38.5 %collective-permute-start.1 = (bf16[1024,256]{1,0:T(8,128)(2,1)S(1)}, bf16[1024,256]{1,0:T(8,128)(2,1)}, u32[]{:S(2)}, u32[]{:S(2)}) collective-permute-start(bf16[1024,256]{1,0:T(8,128)(2,1)S(1)} %copy-done.2), channel_id=1, source_target_pairs={{0,96},{32,0},{64,32},{96,64},{1,97},{33,1},{65,33},{97,65},{2,98}... | collective-permute-start | bytes 1572872 | tf_op jit(solution)/shard_map/ppermute | solution.py:33
  15.8 47.8 %collective-permute-start.4 = (bf16[1024,256]{1,0:T(8,128)(2,1)S(1)}, bf16[1024,256]{1,0:T(8,128)(2,1)S(1)}, u32[]{:S(2)}, u32[]{:S(2)}) collective-permute-start(bf16[1024,256]{1,0:T(8,128)(2,1)S(1)} %copy-done.2), channel_id=1, source_target_pairs={{0,16},{16,0},{1,17},{17,1},{2,18},{18,2},{3,19},{19,3},{4,20},{20... | collective-permute-start | bytes 1572872 | tf_op jit(solution)/shard_map/ppermute | solution.py:33
  54.0 10.4 %collective-permute-start.3 = (bf16[512,256]{1,0:T(8,128)(2,1)S(1)}, bf16[512,256]{1,0:T(8,128)(2,1)}, u32[]{:S(2)}, u32[]{:S(2)}) collective-permute-start(bf16[512,256]{1,0:T(8,128)(2,1)S(1)} %slice.58), channel_id=1, source_target_pairs={{0,96},{32,0},{64,32},{96,64},{1,97},{33,1},{65,33},{97,65},{2,98}... | collective-permute-start | bytes 786440 | tf_op jit(solution)/shard_map/ppermute | solution.py:33
  64.3 19.1 %collective-permute-start.9 = (bf16[1280,256]{1,0:T(8,128)(2,1)}, bf16[1280,256]{1,0:T(8,128)(2,1)S(1)}, u32[]{:S(2)}, u32[]{:S(2)}) collective-permute-start(bf16[1280,256]{1,0:T(8,128)(2,1)} %get-tuple-element.26.refs_0_), channel_id=1, source_target_pairs={{0,32},{32,64},{64,96},{96,0},{1,33},{33,65},{65,97},{97,1},{2,34}... | collective-permute-start | bytes 1966088 | tf_op jit(solution)/shard_map/ppermute | solution.py:33
  64.4 19.2 %collective-permute-start.10 = (bf16[1280,256]{1,0:T(8,128)(2,1)}, bf16[1280,256]{1,0:T(8,128)(2,1)S(1)}, u32[]{:S(2)}, u32[]{:S(2)}) collective-permute-start(bf16[1280,256]{1,0:T(8,128)(2,1)} %get-tuple-element.26.refs_0_), channel_id=1, source_target_pairs={{0,96},{32,0},{64,32},{96,64},{1,97},{33,1},{65,33},{97,65},{2,98}... | collective-permute-start | bytes 1966088 | tf_op jit(solution)/shard_map/ppermute | solution.py:33
  76.2 25.5 %all-to-all-start.1 = ((bf16[16,64,512]{2,1,0:T(8,128)(2,1)}), bf16[16,64,512]{2,1,0:T(8,128)(2,1)}, u32[]{:S(2)}, u32[]{:S(2)}) async-start(bf16[16,64,512]{2,1,0:T(8,128)(2,1)} %bitcast.8), calls=%async_computation.1 | async-start | bytes 2097152 | tf_op jit(solution)/shard_map/all_to_all | solution.py:28
  82.5 12.4 %collective-permute-start.13 = (bf16[1280,256]{1,0:T(8,128)(2,1)}, bf16[1280,256]{1,0:T(8,128)(2,1)S(1)}, u32[]{:S(2)}, u32[]{:S(2)}) collective-permute-start(bf16[1280,256]{1,0:T(8,128)(2,1)} %get-tuple-element.26.refs_0_), channel_id=1, source_target_pairs={{0,16},{16,0},{1,17},{17,1},{2,18},{18,2},{3,19},{19,3},{4,20},{20... | collective-permute-start | bytes 1966088 | tf_op jit(solution)/shard_map/ppermute | solution.py:33
  83.5 10.6 %collective-permute-start.11 = (bf16[640,256]{1,0:T(8,128)(2,1)S(1)}, bf16[640,256]{1,0:T(8,128)(2,1)S(1)}, u32[]{:S(2)}, u32[]{:S(2)}) collective-permute-start(bf16[640,256]{1,0:T(8,128)(2,1)S(1)} %slice.59), channel_id=1, source_target_pairs={{0,32},{32,64},{64,96},{96,0},{1,33},{33,65},{65,97},{97,1},{2,34}... | collective-permute-start | bytes 983048 | tf_op jit(solution)/shard_map/ppermute | solution.py:33
  83.6 11.3 %collective-permute-start.12 = (bf16[640,256]{1,0:T(8,128)(2,1)S(1)}, bf16[640,256]{1,0:T(8,128)(2,1)S(1)}, u32[]{:S(2)}, u32[]{:S(2)}) collective-permute-start(bf16[640,256]{1,0:T(8,128)(2,1)S(1)} %slice.60), channel_id=1, source_target_pairs={{0,96},{32,0},{64,32},{96,64},{1,97},{33,1},{65,33},{97,65},{2,98}... | collective-permute-start | bytes 983048 | tf_op jit(solution)/shard_map/ppermute | solution.py:33
  86.4 10.3 %collective-permute-start.14 = (bf16[1280,256]{1,0:T(8,128)(2,1)S(1)}, bf16[1280,256]{1,0:T(8,128)(2,1)S(1)}, u32[]{:S(2)}, u32[]{:S(2)}) collective-permute-start(bf16[1280,256]{1,0:T(8,128)(2,1)S(1)} %collective-permute-done.9.refs_1_), channel_id=1, source_target_pairs={{0,16},{16,0},{1,17},{17,1},{2,18},{18,2},{3,19},{19,3},{4,20},{20... | collective-permute-start | bytes 1966088 | tf_op jit(solution)/shard_map/ppermute | solution.py:33
  101.7 51.0 %all-to-all-start.2 = ((bf16[16,80,512]{2,1,0:T(8,128)(2,1)}), bf16[16,80,512]{2,1,0:T(8,128)(2,1)}, u32[]{:S(2)}, u32[]{:S(2)}) async-start(bf16[16,80,512]{2,1,0:T(8,128)(2,1)} %bitcast.9), calls=%async_computation.2 | async-start | bytes 2621440 | tf_op jit(solution)/shard_map/all_to_all | solution.py:28
  109.3 22.1 %collective-permute-start.18 = (bf16[272,256]{1,0:T(8,128)(2,1)S(1)}, bf16[272,256]{1,0:T(8,128)(2,1)S(1)}, u32[]{:S(2)}, u32[]{:S(2)}) collective-permute-start(bf16[272,256]{1,0:T(8,128)(2,1)S(1)} %get-tuple-element.27), channel_id=1, source_target_pairs={{0,1},{1,2},{2,3},{3,0},{4,5},{5,6},{6,7},{7,4},{8,9},{9,10},{10,1... | collective-permute-start | bytes 417800 | tf_op jit(solution)/shard_map/ppermute | solution.py:33
  110.3 21.2 %collective-permute-start.19 = (bf16[272,256]{1,0:T(8,128)(2,1)S(1)}, bf16[272,256]{1,0:T(8,128)(2,1)S(1)}, u32[]{:S(2)}, u32[]{:S(2)}) collective-permute-start(bf16[272,256]{1,0:T(8,128)(2,1)S(1)} %get-tuple-element.27), channel_id=1, source_target_pairs={{0,2},{1,3},{2,0},{3,1},{4,6},{5,7},{6,4},{7,5},{8,10},{9,11},{10,... | collective-permute-start | bytes 417800 | tf_op jit(solution)/shard_map/ppermute | solution.py:33
  110.9 20.6 %collective-permute-start.20 = (bf16[272,256]{1,0:T(8,128)(2,1)S(1)}, bf16[272,256]{1,0:T(8,128)(2,1)S(1)}, u32[]{:S(2)}, u32[]{:S(2)}) collective-permute-start(bf16[272,256]{1,0:T(8,128)(2,1)S(1)} %get-tuple-element.27), channel_id=1, source_target_pairs={{0,3},{1,0},{2,1},{3,2},{4,7},{5,4},{6,5},{7,6},{8,11},{9,8},{10,9... | collective-permute-start | bytes 417800 | tf_op jit(solution)/shard_map/ppermute | solution.py:33
  131.6 19.7 %collective-permute-start.21 = (bf16[4,272,256]{2,1,0:T(8,128)(2,1)S(1)}, bf16[4,272,256]{2,1,0:T(8,128)(2,1)S(1)}, u32[]{:S(2)}, u32[]{:S(2)}) collective-permute-start(bf16[4,272,256]{2,1,0:T(8,128)(2,1)S(1)} %pad_maximum_fusion.refs_1_.refs_2_.refs_5_), channel_id=1, source_target_pairs={{0,4},{4,8},{8,12},{12,0},{1,5},{5,9},{9,13},{13,1},{2,6},{6,10},{... | collective-permute-start | bytes 1671176 | tf_op jit(solution)/shard_map/ppermute | solution.py:33
  132.5 15.8 %collective-permute-start.24 = (bf16[272,256]{1,0:T(8,128)(2,1)S(1)}, bf16[272,256]{1,0:T(8,128)(2,1)S(1)}, u32[]{:S(2)}, u32[]{:S(2)}) collective-permute-start(bf16[272,256]{1,0:T(8,128)(2,1)S(1)} %get-tuple-element.28), channel_id=1, source_target_pairs={{0,4},{4,8},{8,12},{12,0},{1,5},{5,9},{9,13},{13,1},{2,6},{6,10},{... | collective-permute-start | bytes 417800 | tf_op jit(solution)/shard_map/ppermute | solution.py:33
  133.1 16.5 %collective-permute-start.25 = (bf16[272,256]{1,0:T(8,128)(2,1)S(1)}, bf16[272,256]{1,0:T(8,128)(2,1)S(1)}, u32[]{:S(2)}, u32[]{:S(2)}) collective-permute-start(bf16[272,256]{1,0:T(8,128)(2,1)S(1)} %get-tuple-element.28), channel_id=1, source_target_pairs={{0,8},{4,12},{8,0},{12,4},{1,9},{5,13},{9,1},{13,5},{2,10},{6,14},... | collective-permute-start | bytes 417800 | tf_op jit(solution)/shard_map/ppermute | solution.py:33
  134.9 14.7 %collective-permute-start.26 = (bf16[272,256]{1,0:T(8,128)(2,1)S(1)}, bf16[272,256]{1,0:T(8,128)(2,1)S(1)}, u32[]{:S(2)}, u32[]{:S(2)}) collective-permute-start(bf16[272,256]{1,0:T(8,128)(2,1)S(1)} %get-tuple-element.28), channel_id=1, source_target_pairs={{0,12},{4,0},{8,4},{12,8},{1,13},{5,1},{9,5},{13,9},{2,14},{6,2},{... | collective-permute-start | bytes 417800 | tf_op jit(solution)/shard_map/ppermute | solution.py:33
  135.2 19.0 %collective-permute-start.22 = (bf16[4,272,256]{2,1,0:T(8,128)(2,1)S(1)}, bf16[4,272,256]{2,1,0:T(8,128)(2,1)S(1)}, u32[]{:S(2)}, u32[]{:S(2)}) collective-permute-start(bf16[4,272,256]{2,1,0:T(8,128)(2,1)S(1)} %pad_maximum_fusion.refs_1_.refs_2_.refs_5_), channel_id=1, source_target_pairs={{0,8},{4,12},{8,0},{12,4},{1,9},{5,13},{9,1},{13,5},{2,10},{6,14},... | collective-permute-start | bytes 1671176 | tf_op jit(solution)/shard_map/ppermute | solution.py:33
  148.3 18.2 %collective-permute-start.23 = (bf16[4,272,256]{2,1,0:T(8,128)(2,1)S(1)}, bf16[4,272,256]{2,1,0:T(8,128)(2,1)S(1)}, u32[]{:S(2)}, u32[]{:S(2)}) collective-permute-start(bf16[4,272,256]{2,1,0:T(8,128)(2,1)S(1)} %pad_maximum_fusion.refs_1_.refs_2_.refs_5_), channel_id=1, source_target_pairs={{0,12},{4,0},{8,4},{12,8},{1,13},{5,1},{9,5},{13,9},{2,14},{6,2},{... | collective-permute-start | bytes 1671176 | tf_op jit(solution)/shard_map/ppermute | solution.py:33
  149.6 17.7 %collective-permute-start.27 = (bf16[4,272,256]{2,1,0:T(8,128)(2,1)S(1)}, bf16[4,272,256]{2,1,0:T(8,128)(2,1)S(1)}, u32[]{:S(2)}, u32[]{:S(2)}) collective-permute-start(bf16[4,272,256]{2,1,0:T(8,128)(2,1)S(1)} %pad_maximum_fusion.1.refs_5_.refs_6_.refs_9_), channel_id=1, source_target_pairs={{0,1},{1,2},{2,3},{3,0},{4,5},{5,6},{6,7},{7,4},{8,9},{9,10},{10,1... | collective-permute-start | bytes 1671176 | tf_op jit(solution)/shard_map/ppermute | solution.py:33
  149.7 19.1 %collective-permute-start.28 = (bf16[4,272,256]{2,1,0:T(8,128)(2,1)S(1)}, bf16[4,272,256]{2,1,0:T(8,128)(2,1)}, u32[]{:S(2)}, u32[]{:S(2)}) collective-permute-start(bf16[4,272,256]{2,1,0:T(8,128)(2,1)S(1)} %pad_maximum_fusion.1.refs_5_.refs_6_.refs_9_), channel_id=1, source_target_pairs={{0,2},{1,3},{2,0},{3,1},{4,6},{5,7},{6,4},{7,5},{8,10},{9,11},{10,... | collective-permute-start | bytes 1671176 | tf_op jit(solution)/shard_map/ppermute | solution.py:33
  151.2 35.5 %collective-permute-start.29 = (bf16[4,272,256]{2,1,0:T(8,128)(2,1)S(1)}, bf16[4,272,256]{2,1,0:T(8,128)(2,1)}, u32[]{:S(2)}, u32[]{:S(2)}) collective-permute-start(bf16[4,272,256]{2,1,0:T(8,128)(2,1)S(1)} %pad_maximum_fusion.1.refs_5_.refs_6_.refs_9_), channel_id=1, source_target_pairs={{0,3},{1,0},{2,1},{3,2},{4,7},{5,4},{6,5},{7,6},{8,11},{9,8},{10,9... | collective-permute-start | bytes 1671176 | tf_op jit(solution)/shard_map/ppermute | solution.py:33
  154.2 29.8 %collective-permute-start.30 = (bf16[144,512]{1,0:T(8,128)(2,1)S(1)}, bf16[144,512]{1,0:T(8,128)(2,1)S(1)}, u32[]{:S(2)}, u32[]{:S(2)}) collective-permute-start(bf16[144,512]{1,0:T(8,128)(2,1)S(1)} %fusion.2.refs_9_), channel_id=1, source_target_pairs={{0,32},{32,64},{64,96},{96,0},{1,33},{33,65},{65,97},{97,1},{2,34}... | collective-permute-start | bytes 442376 | tf_op jit(solution)/shard_map/ppermute | solution.py:33
  166.5 17.6 %collective-permute-start.31 = (bf16[144,512]{1,0:T(8,128)(2,1)S(1)}, bf16[144,512]{1,0:T(8,128)(2,1)S(1)}, u32[]{:S(2)}, u32[]{:S(2)}) collective-permute-start(bf16[144,512]{1,0:T(8,128)(2,1)S(1)} %fusion.2.refs_9_), channel_id=1, source_target_pairs={{0,64},{32,96},{64,0},{96,32},{1,65},{33,97},{65,1},{97,33},{2,66}... | collective-permute-start | bytes 442376 | tf_op jit(solution)/shard_map/ppermute | solution.py:33
  167.3 17.2 %collective-permute-start.32 = (bf16[144,512]{1,0:T(8,128)(2,1)S(1)}, bf16[144,512]{1,0:T(8,128)(2,1)S(1)}, u32[]{:S(2)}, u32[]{:S(2)}) collective-permute-start(bf16[144,512]{1,0:T(8,128)(2,1)S(1)} %fusion.2.refs_9_), channel_id=1, source_target_pairs={{0,96},{32,0},{64,32},{96,64},{1,97},{33,1},{65,33},{97,65},{2,98}... | collective-permute-start | bytes 442376 | tf_op jit(solution)/shard_map/ppermute | solution.py:33
  168.8 17.9 %collective-permute-start.33 = (bf16[144,512]{1,0:T(8,128)(2,1)S(1)}, bf16[144,512]{1,0:T(8,128)(2,1)S(1)}, u32[]{:S(2)}, u32[]{:S(2)}) collective-permute-start(bf16[144,512]{1,0:T(8,128)(2,1)S(1)} %fusion.2.refs_9_), channel_id=1, source_target_pairs={{0,16},{16,0},{1,17},{17,1},{2,18},{18,2},{3,19},{19,3},{4,20},{20... | collective-permute-start | bytes 442376 | tf_op jit(solution)/shard_map/ppermute | solution.py:33
  192.0 12.0 %collective-permute-start.38 = (bf16[160,512]{1,0:T(8,128)(2,1)S(1)}, bf16[160,512]{1,0:T(8,128)(2,1)S(1)}, u32[]{:S(2)}, u32[]{:S(2)}) collective-permute-start(bf16[160,512]{1,0:T(8,128)(2,1)S(1)} %get-tuple-element.30.refs_10_), channel_id=1, source_target_pairs={{0,64},{32,96},{64,0},{96,32},{1,65},{33,97},{65,1},{97,33},{2,66}... | collective-permute-start | bytes 491528 | tf_op jit(solution)/shard_map/ppermute | solution.py:33
  241.9 20.3 %collective-permute-start.58 = (f32[144,256]{1,0:T(8,128)S(1)}, f32[144,256]{1,0:T(8,128)S(1)}, u32[]{:S(2)}, u32[]{:S(2)}) collective-permute-start(f32[144,256]{1,0:T(8,128)S(1)} %get-tuple-element.41), channel_id=1, source_target_pairs={{0,0},{1,1},{2,16},{3,17},{4,32},{5,33},{6,48},{7,49},{8,64},{9,65... | collective-permute-start | bytes 442376 | tf_op jit(solution)/shard_map/ppermute | solution.py:335
  243.9 18.3 %collective-permute-start.59 = (f32[144,256]{1,0:T(8,128)S(1)}, f32[144,256]{1,0:T(8,128)S(1)}, u32[]{:S(2)}, u32[]{:S(2)}) collective-permute-start(f32[144,256]{1,0:T(8,128)S(1)} %get-tuple-element.42), channel_id=1, source_target_pairs={{0,1},{1,0},{2,17},{3,16},{4,33},{5,32},{6,49},{7,48},{8,65},{9,64... | collective-permute-start | bytes 442376 | tf_op jit(solution)/shard_map/ppermute | solution.py:335
  (37 other events, 225.5 us)

commit v2 on v1

--- a/solution.py
+++ b/solution.py
@@ -137,10 +137,10 @@
     return out
 
 
-def gather_weights(piece):
+def gather_weights(piece, split):
     middle = piece.shape[0] // 2
     up, down = turn(piece, "y", 1), turn(piece, "y", 3)
-    far = [turn(up[:middle], "y", 1), turn(down[middle:], "y", 3)]
+    far = [turn(up[:middle], "y", 1), turn(down[middle:], "y", 3)] if split else [turn(down, "y", 3)]
     others = [turn(b, "core", 1) for b in (piece, up, down)]
     others += [turn(b, "core", 1) for b in far]
     return [piece, up, down] + far + others
@@ -157,11 +157,13 @@
     for part in range(2):
         rows = slice(part * middle, (part + 1) * middle)
         total = jnp.zeros((middle, out_ref.shape[1]), F32)
+        count = len(blocks) // 2
         for other in range(2):
-            five = blocks[5 * other : 5 * other + 5]
+            some = blocks[count * other : count * other + count]
             for k in range(3):
-                total += dot(five[k][rows], grams[4 * other + k][:ROWS])
-            total += dot(five[3 + part][...], grams[4 * other + 3][:ROWS])
+                total += dot(some[k][rows], grams[4 * other + k][:ROWS])
+            far = some[3 + part][...] if count == 5 else some[3][rows]
+            total += dot(far, grams[4 * other + 3][:ROWS])
         out_ref[rows] = total.astype(BF16)
 
 
@@ -179,7 +181,9 @@
 
 
 def gather(block):
-    mine = [block] + [turn(block, "y", step) for step in (1, 2, 3)]
+    mine = [block]
+    for step in (1, 2, 3):
+        mine.append(turn(block, "y", step))
     return mine + [turn(b, "core", 1) for b in mine]
 
 
@@ -345,12 +349,12 @@
     pos = jnp.stack([jnp.asarray(p, jnp.int32) for p in pos])
 
     pieces = transposed(member_weights[0])
-    early = gather_weights(pieces[0])
+    early = gather_weights(pieces[0], True)
     ready, pieces = lax.optimization_barrier((pos, pieces))
     spread = spread_grams(ready, member_grams[0])
     grams = exchange(spread, MEMBER)
     late, grams = lax.optimization_barrier((pieces[1], grams))
-    late = gather_weights(late)
+    late = gather_weights(late, False)
     gram_sum = gather_plane([gather_line(half, axis) for half, axis in zip(sum_grams(pos, grams), ("x", "z"))])
     parts = []
     for piece, blocks in zip(PIECES, (early, late)):

time: 264 us -> 270 us (1.023)
  the two profiles are of different devices: /device:TPU:101 before, /device:TPU:24 now
where the time goes in v2:
time: 270 us; the launch traced here: 265 us
  waiting for transfers between devices  148 us (55%)
  starting transfers between devices  76.7 us (28%)
  Pallas kernels  31.7 us (12%)
  other arithmetic  6.21 us (2%)
    ppermute x56, waiting for transfers between devices, turn(): lax.ppermute(block, axis, [(i, (i + step) % size) for i in range(size)])  105 us
    ppermute x56, starting transfers between devices, turn(): lax.ppermute(block, axis, [(i, (i + step) % size) for i in range(size)])  42.2 us
    all_to_all x3, waiting for transfers between devices, exchange(): return lax.all_to_all(parts, axis, split_axis=0, concat_axis=0, tiled=True)  32.2 us
    all_to_all x3, starting transfers between devices, exchange(): return lax.all_to_all(parts, axis, split_axis=0, concat_axis=0, tiled=True)  17.3 us
    ppermute x2, starting transfers between devices, to_output(): came.append(lax.ppermute(sent, ALL, pairs))  17.2 us
    pallas_call x3, Pallas kernels, run(): pl.pallas_call(kernel, in_specs=[SMEM] + [VMEM] * (len(owns) + len(grams)...  13.6 us
    ppermute x2, waiting for transfers between devices, to_output(): came.append(lax.ppermute(sent, ALL, pairs))  10.8 us
    pallas_call x2, Pallas kernels, right_side_part(): pl.pallas_call(right_side_kernel, in_specs=[SMEM, VMEM] + [VMEM] * len(bl...  9.97 us
  transfers between devices with their start and end apart: 61, of which 33 were waited for; matrix products, arithmetic and copies ran while one was open for 1% of the time, Pallas kernels for 4%

profile of v2, /device:TPU:24, one launch (start us, length us, event | category | flops | bytes accessed | tf_op | source)
XLA Modules:
  0.0 265.3 jit_solution(1619207086519689557)
XLA Ops:
  0.0 2.4 turn_weights.1
  3.0 4.8 %spread_grams.1 = bf16[8,272,512]{2,1,0:T(8,128)(2,1)} custom-call(s32[8]{0:T(128)} %stack.57.pos_ref, f32[256,4096]{1,0:T(8,128)} %bitcast.36), custom_call_target="tpu_custom_call" | custom-call | flops 100000000 | bytes 6291456 | tf_op jit(solution)/shard_map/spread_grams/pallas_call | solution.py:88
  7.8 4.8 %all-to-all-start = ((bf16[8,272,512]{2,1,0:T(8,128)(2,1)}), bf16[8,272,512]{2,1,0:T(8,128)(2,1)S(1)}, u32[]{:S(2)}, u32[]{:S(2)}) async-start(bf16[8,272,512]{2,1,0:T(8,128)(2,1)} %spread_grams.1), calls=%async_computation | async-start | bytes 4456448 | tf_op jit(solution)/shard_map/all_to_all | solution.py:28
  14.6 25.1 %all-to-all-done.g_ref.blocks_ref = bf16[8,272,512]{2,1,0:T(8,128)(2,1)S(1)} async-done(((bf16[8,272,512]{2,1,0:T(8,128)(2,1)}), bf16[8,272,512]{2,1,0:T(8,128)(2,1)S(1)}, u32[]{:S(2)}, u32[]{:S(2)}) %all-to-all-start) | async-done | bytes 2228256 | tf_op jit(solution)/shard_map/all_to_all | solution.py:28
  39.7 10.1 %collective-permute-done.refs_1_ = bf16[1024,256]{1,0:T(8,128)(2,1)S(1)} collective-permute-done((bf16[1024,256]{1,0:T(8,128)(2,1)}, bf16[1024,256]{1,0:T(8,128)(2,1)S(1)}, u32[]{:S(2)}, u32[]{:S(2)}) %collective-permute-start) | collective-permute-done | bytes 524320 | tf_op jit(solution)/shard_map/ppermute | solution.py:33
  49.8 2.4 collective-permute-start.2
  52.3 5.3 %collective-permute-done.2.refs_3_ = bf16[512,256]{1,0:T(8,128)(2,1)S(1)} collective-permute-done((bf16[512,256]{1,0:T(8,128)(2,1)S(1)}, bf16[512,256]{1,0:T(8,128)(2,1)S(1)}, u32[]{:S(2)}, u32[]{:S(2)}) %collective-permute-start.2) | collective-permute-done | bytes 262176 | tf_op jit(solution)/shard_map/ppermute | solution.py:33
  58.2 10.8 %collective-permute-done.3.refs_4_ = bf16[512,256]{1,0:T(8,128)(2,1)S(1)} collective-permute-done((bf16[512,256]{1,0:T(8,128)(2,1)S(1)}, bf16[512,256]{1,0:T(8,128)(2,1)S(1)}, u32[]{:S(2)}, u32[]{:S(2)}) %collective-permute-start.3) | collective-permute-done | bytes 262176 | tf_op jit(solution)/shard_map/ppermute | solution.py:33
  72.5 4.5 %right_side.2 = bf16[1024,512]{1,0:T(8,128)(2,1)} custom-call(s32[8]{0:T(128)S(1)} %copy-done.1, bf16[8,272,512]{2,1,0:T(8,128)(2,1)S(1)} %all-to-all-done.g_ref.blocks_ref, bf16[1024,256]{1,0:T(8,128)(2,1)} %get-tuple-element.21.refs_0_, bf16[1024,256]{1,0:T(8,128)(2,1)S(1)} %collective-permute-done.refs_1_, ...), custom_call_target="tpu_custom_call" | custom-call | flops 2147483648 | bytes 7471104 | tf_op jit(solution)/shard_map/right_side/pallas_call | solution.py:172
  77.1 8.1 %all-to-all-start.1 = ((bf16[16,64,512]{2,1,0:T(8,128)(2,1)}), bf16[16,64,512]{2,1,0:T(8,128)(2,1)}, u32[]{:S(2)}, u32[]{:S(2)}) async-start(bf16[16,64,512]{2,1,0:T(8,128)(2,1)} %bitcast.8), calls=%async_computation.1 | async-start | bytes 2097152 | tf_op jit(solution)/shard_map/all_to_all | solution.py:28
  90.4 5.5 %right_side.3 = bf16[1280,512]{1,0:T(8,128)(2,1)} custom-call(s32[8]{0:T(128)S(1)} %copy-done.1, bf16[8,272,512]{2,1,0:T(8,128)(2,1)S(1)} %all-to-all-done.g_ref.blocks_ref, bf16[1280,256]{1,0:T(8,128)(2,1)S(1)} %copy-done.2, bf16[1280,256]{1,0:T(8,128)(2,1)} %collective-permute-done.9.refs_1_, bf16[1280,256]{1,0:T(8,128)(2,1)} %collective-permute-done.10.refs_2_, ...), custom_call_target="tpu_custom_call" | custom-call | flops 2684354560 | bytes 8781824 | tf_op jit(solution)/shard_map/right_side/pallas_call | solution.py:172
  95.8 7.2 %all-to-all-done.1 = bf16[16,64,512]{2,1,0:T(8,128)(2,1)} async-done(((bf16[16,64,512]{2,1,0:T(8,128)(2,1)}), bf16[16,64,512]{2,1,0:T(8,128)(2,1)}, u32[]{:S(2)}, u32[]{:S(2)}) %all-to-all-start.1) | async-done | bytes 1048608 | tf_op jit(solution)/shard_map/all_to_all | solution.py:28
  103.0 4.4 %all-to-all-start.2 = ((bf16[16,80,512]{2,1,0:T(8,128)(2,1)}), bf16[16,80,512]{2,1,0:T(8,128)(2,1)}, u32[]{:S(2)}, u32[]{:S(2)}) async-start(bf16[16,80,512]{2,1,0:T(8,128)(2,1)} %bitcast.9), calls=%async_computation.2 | async-start | bytes 2621440 | tf_op jit(solution)/shard_map/all_to_all | solution.py:28
  110.2 2.7 %collective-permute-start.17 = (bf16[272,256]{1,0:T(8,128)(2,1)S(1)}, bf16[272,256]{1,0:T(8,128)(2,1)S(1)}, u32[]{:S(2)}, u32[]{:S(2)}) collective-permute-start(bf16[272,256]{1,0:T(8,128)(2,1)S(1)} %get-tuple-element.27), channel_id=1, source_target_pairs={{0,2},{1,3},{2,0},{3,1},{4,6},{5,7},{6,4},{7,5},{8,10},{9,11},{10,... | collective-permute-start | bytes 417800 | tf_op jit(solution)/shard_map/ppermute | solution.py:33
  114.3 14.0 %collective-permute-done.16 = bf16[272,256]{1,0:T(8,128)(2,1)S(1)} collective-permute-done((bf16[272,256]{1,0:T(8,128)(2,1)S(1)}, bf16[272,256]{1,0:T(8,128)(2,1)S(1)}, u32[]{:S(2)}, u32[]{:S(2)}) %collective-permute-start.16) | collective-permute-done | bytes 139296 | tf_op jit(solution)/shard_map/ppermute | solution.py:33
  138.0 11.4 %collective-permute-done.22 = bf16[272,256]{1,0:T(8,128)(2,1)S(1)} collective-permute-done((bf16[272,256]{1,0:T(8,128)(2,1)S(1)}, bf16[272,256]{1,0:T(8,128)(2,1)S(1)}, u32[]{:S(2)}, u32[]{:S(2)}) %collective-permute-start.22) | collective-permute-done | bytes 139296 | tf_op jit(solution)/shard_map/ppermute | solution.py:33
  151.5 2.4 collective-permute-done.23
  162.8 2.9 %collective-permute-start.28 = (bf16[144,512]{1,0:T(8,128)(2,1)S(1)}, bf16[144,512]{1,0:T(8,128)(2,1)S(1)}, u32[]{:S(2)}, u32[]{:S(2)}) collective-permute-start(bf16[144,512]{1,0:T(8,128)(2,1)S(1)} %fusion.2.refs_9_), channel_id=1, source_target_pairs={{0,32},{32,64},{64,96},{96,0},{1,33},{33,65},{65,97},{97,1},{2,34}... | collective-permute-start | bytes 442376 | tf_op jit(solution)/shard_map/ppermute | solution.py:33
  166.5 10.2 %collective-permute-done.25.refs_6_.refs_7_.refs_10_ = bf16[4,272,256]{2,1,0:T(8,128)(2,1)S(1)} collective-permute-done((bf16[4,272,256]{2,1,0:T(8,128)(2,1)S(1)}, bf16[4,272,256]{2,1,0:T(8,128)(2,1)S(1)}, u32[]{:S(2)}, u32[]{:S(2)}) %collective-permute-start.25) | collective-permute-done | bytes 557088 | tf_op jit(solution)/shard_map/ppermute | solution.py:33
  179.0 4.1 %collective-permute-done.30.refs_12_ = bf16[144,512]{1,0:T(8,128)(2,1)S(1)} collective-permute-done((bf16[144,512]{1,0:T(8,128)(2,1)S(1)}, bf16[144,512]{1,0:T(8,128)(2,1)S(1)}, u32[]{:S(2)}, u32[]{:S(2)}) %collective-permute-start.30) | collective-permute-done | bytes 147488 | tf_op jit(solution)/shard_map/ppermute | solution.py:33
  184.5 4.2 %shard_map.28 = (f32[144,512]{1,0:T(8,128)S(1)}, bf16[160,512]{1,0:T(8,128)(2,1)S(1)}) custom-call(s32[8]{0:T(128)S(1)} %copy-done.1, f32[144,512]{1,0:T(8,128)S(1)} %pad_maximum_fusion.2.refs_0_, bf16[4,272,256]{2,1,0:T(8,128)(2,1)S(1)} %pad_maximum_fusion.refs_1_.refs_2_.refs_5_, bf16[4,272,256]{2,1,0:T(8,128)(2,1)S(1)} %collective-permute-done.19.refs_2_.refs_3_.refs_6_, ...), custom_call_target="tpu_custom_call" | custom-call | flops 603979776 | bytes 4194304 | tf_op jit(solution)/shard_map/pallas_call | solution.py:317
  191.5 4.3 %collective-permute-done.35.refs_11_ = bf16[160,512]{1,0:T(8,128)(2,1)S(1)} collective-permute-done((bf16[160,512]{1,0:T(8,128)(2,1)S(1)}, bf16[160,512]{1,0:T(8,128)(2,1)S(1)}, u32[]{:S(2)}, u32[]{:S(2)}) %collective-permute-start.35) | collective-permute-done | bytes 163872 | tf_op jit(solution)/shard_map/ppermute | solution.py:33
  195.9 3.2 %collective-permute-done.36.refs_12_ = bf16[160,512]{1,0:T(8,128)(2,1)S(1)} collective-permute-done((bf16[160,512]{1,0:T(8,128)(2,1)S(1)}, bf16[160,512]{1,0:T(8,128)(2,1)S(1)}, u32[]{:S(2)}, u32[]{:S(2)}) %collective-permute-start.36) | collective-permute-done | bytes 163872 | tf_op jit(solution)/shard_map/ppermute | solution.py:33
  199.1 2.4 collective-permute-done.37.refs_13_
  202.9 4.5 %shard_map.29 = (f32[144,768]{1,0:T(8,128)S(1)}, f32[144,512]{1,0:T(8,128)S(1)}, f32[144,512]{1,0:T(8,128)S(1)}, bf16[160,512]{1,0:T(8,128)(2,1)S(1)}) custom-call(s32[8]{0:T(128)S(1)} %copy-done.1, f32[144,512]{1,0:T(8,128)S(1)} %pad_maximum_fusion.2.refs_0_, f32[144,512]{1,0:T(8,128)S(1)} %get-tuple-element.29.refs_1_, ...), custom_call_target="tpu_custom_call" | custom-call | flops 603979776 | bytes 4194304 | tf_op jit(solution)/shard_map/pallas_call | solution.py:317
  209.7 4.8 %collective-permute-done.42.refs_14_ = bf16[160,512]{1,0:T(8,128)(2,1)S(1)} collective-permute-done((bf16[160,512]{1,0:T(8,128)(2,1)S(1)}, bf16[160,512]{1,0:T(8,128)(2,1)S(1)}, u32[]{:S(2)}, u32[]{:S(2)}) %collective-permute-start.42) | collective-permute-done | bytes 163872 | tf_op jit(solution)/shard_map/ppermute | solution.py:33
  216.6 2.4 collective-permute-done.44.refs_16_
  220.4 4.9 %shard_map.30 = (f32[144,1792]{1,0:T(8,128)S(1)}, f32[8,1,288]{2,1,0:T(1,128)S(1)}) custom-call(s32[8]{0:T(128)S(1)} %copy-done.1, f32[144,512]{1,0:T(8,128)S(1)} %pad_maximum_fusion.2.refs_0_, f32[144,512]{1,0:T(8,128)S(1)} %get-tuple-element.29.refs_1_, f32[144,768]{1,0:T(8,128)S(1)} %get-tuple-element.31.refs_2_, ...), custom_call_target="tpu_custom_call" | custom-call | flops 603979776 | bytes 4194304 | tf_op jit(solution)/shard_map/pallas_call | solution.py:317
  226.3 2.5 collective-permute-start.50
  236.4 14.3 %collective-permute-start.56 = (f32[144,256]{1,0:T(8,128)S(1)}, f32[144,256]{1,0:T(8,128)S(1)}, u32[]{:S(2)}, u32[]{:S(2)}) collective-permute-start(f32[144,256]{1,0:T(8,128)S(1)} %get-tuple-element.41), channel_id=1, source_target_pairs={{0,0},{1,1},{2,16},{3,17},{4,32},{5,33},{6,48},{7,49},{8,64},{9,65... | collective-permute-start | bytes 442376 | tf_op jit(solution)/shard_map/ppermute | solution.py:339
  250.8 2.9 %collective-permute-start.57 = (f32[144,256]{1,0:T(8,128)S(1)}, f32[144,256]{1,0:T(8,128)S(1)}, u32[]{:S(2)}, u32[]{:S(2)}) collective-permute-start(f32[144,256]{1,0:T(8,128)S(1)} %get-tuple-element.42), channel_id=1, source_target_pairs={{0,1},{1,0},{2,17},{3,16},{4,33},{5,32},{6,49},{7,48},{8,65},{9,64... | collective-permute-start | bytes 442376 | tf_op jit(solution)/shard_map/ppermute | solution.py:339
  253.7 10.8 %collective-permute-done.56 = f32[144,256]{1,0:T(8,128)S(1)} collective-permute-done((f32[144,256]{1,0:T(8,128)S(1)}, f32[144,256]{1,0:T(8,128)S(1)}, u32[]{:S(2)}, u32[]{:S(2)}) %collective-permute-start.56) | collective-permute-done | bytes 147488 | tf_op jit(solution)/shard_map/ppermute | solution.py:339
  (122 shorter events, 60.8 us)
Async XLA Ops:
  7.8 31.9 %all-to-all-start = ((bf16[8,272,512]{2,1,0:T(8,128)(2,1)}), bf16[8,272,512]{2,1,0:T(8,128)(2,1)S(1)}, u32[]{:S(2)}, u32[]{:S(2)}) async-start(bf16[8,272,512]{2,1,0:T(8,128)(2,1)} %spread_grams.1), calls=%async_computation | async-start | bytes 4456448 | tf_op jit(solution)/shard_map/all_to_all | solution.py:28
  12.6 37.2 %collective-permute-start = (bf16[1024,256]{1,0:T(8,128)(2,1)}, bf16[1024,256]{1,0:T(8,128)(2,1)S(1)}, u32[]{:S(2)}, u32[]{:S(2)}) collective-permute-start(bf16[1024,256]{1,0:T(8,128)(2,1)} %get-tuple-element.21.refs_0_), channel_id=1, source_target_pairs={{0,32},{32,64},{64,96},{96,0},{1,33},{33,65},{65,97},{97,1},{2,34}... | collective-permute-start | bytes 1572872 | tf_op jit(solution)/shard_map/ppermute | solution.py:33
  12.6 39.6 %collective-permute-start.1 = (bf16[1024,256]{1,0:T(8,128)(2,1)}, bf16[1024,256]{1,0:T(8,128)(2,1)S(1)}, u32[]{:S(2)}, u32[]{:S(2)}) collective-permute-start(bf16[1024,256]{1,0:T(8,128)(2,1)} %get-tuple-element.21.refs_0_), channel_id=1, source_target_pairs={{0,96},{32,0},{64,32},{96,64},{1,97},{33,1},{65,33},{97,65},{2,98}... | collective-permute-start | bytes 1572872 | tf_op jit(solution)/shard_map/ppermute | solution.py:33
  14.6 43.5 %collective-permute-start.4 = (bf16[1024,256]{1,0:T(8,128)(2,1)}, bf16[1024,256]{1,0:T(8,128)(2,1)}, u32[]{:S(2)}, u32[]{:S(2)}) collective-permute-start(bf16[1024,256]{1,0:T(8,128)(2,1)} %get-tuple-element.21.refs_0_), channel_id=1, source_target_pairs={{0,16},{16,0},{1,17},{17,1},{2,18},{18,2},{3,19},{19,3},{4,20},{20... | collective-permute-start | bytes 1572872 | tf_op jit(solution)/shard_map/ppermute | solution.py:33
  39.7 30.9 %collective-permute-start.10 = (bf16[1280,256]{1,0:T(8,128)(2,1)}, bf16[1280,256]{1,0:T(8,128)(2,1)}, u32[]{:S(2)}, u32[]{:S(2)}) collective-permute-start(bf16[1280,256]{1,0:T(8,128)(2,1)} %get-tuple-element.26.refs_0_), channel_id=1, source_target_pairs={{0,96},{32,0},{64,32},{96,64},{1,97},{33,1},{65,33},{97,65},{2,98}... | collective-permute-start | bytes 1966088 | tf_op jit(solution)/shard_map/ppermute | solution.py:33
  52.2 16.7 %collective-permute-start.3 = (bf16[512,256]{1,0:T(8,128)(2,1)S(1)}, bf16[512,256]{1,0:T(8,128)(2,1)S(1)}, u32[]{:S(2)}, u32[]{:S(2)}) collective-permute-start(bf16[512,256]{1,0:T(8,128)(2,1)S(1)} %slice.50), channel_id=1, source_target_pairs={{0,96},{32,0},{64,32},{96,64},{1,97},{33,1},{65,33},{97,65},{2,98}... | collective-permute-start | bytes 786440 | tf_op jit(solution)/shard_map/ppermute | solution.py:33
  57.7 13.3 %collective-permute-start.7 = (bf16[512,256]{1,0:T(8,128)(2,1)S(1)}, bf16[512,256]{1,0:T(8,128)(2,1)S(1)}, u32[]{:S(2)}, u32[]{:S(2)}) collective-permute-start(bf16[512,256]{1,0:T(8,128)(2,1)S(1)} %collective-permute-done.2.refs_3_), channel_id=1, source_target_pairs={{0,16},{16,0},{1,17},{17,1},{2,18},{18,2},{3,19},{19,3},{4,20},{20... | collective-permute-start | bytes 786440 | tf_op jit(solution)/shard_map/ppermute | solution.py:33
  57.7 14.8 %collective-permute-start.5 = (bf16[1024,256]{1,0:T(8,128)(2,1)S(1)}, bf16[1024,256]{1,0:T(8,128)(2,1)S(1)}, u32[]{:S(2)}, u32[]{:S(2)}) collective-permute-start(bf16[1024,256]{1,0:T(8,128)(2,1)S(1)} %collective-permute-done.refs_1_), channel_id=1, source_target_pairs={{0,16},{16,0},{1,17},{17,1},{2,18},{18,2},{3,19},{19,3},{4,20},{20... | collective-permute-start | bytes 1572872 | tf_op jit(solution)/shard_map/ppermute | solution.py:33
  58.2 14.3 %collective-permute-start.6 = (bf16[1024,256]{1,0:T(8,128)(2,1)S(1)}, bf16[1024,256]{1,0:T(8,128)(2,1)S(1)}, u32[]{:S(2)}, u32[]{:S(2)}) collective-permute-start(bf16[1024,256]{1,0:T(8,128)(2,1)S(1)} %collective-permute-done.1.refs_2_), channel_id=1, source_target_pairs={{0,16},{16,0},{1,17},{17,1},{2,18},{18,2},{3,19},{19,3},{4,20},{20... | collective-permute-start | bytes 1572872 | tf_op jit(solution)/shard_map/ppermute | solution.py:33
  69.0 16.9 %collective-permute-start.9 = (bf16[1280,256]{1,0:T(8,128)(2,1)}, bf16[1280,256]{1,0:T(8,128)(2,1)}, u32[]{:S(2)}, u32[]{:S(2)}) collective-permute-start(bf16[1280,256]{1,0:T(8,128)(2,1)} %get-tuple-element.26.refs_0_), channel_id=1, source_target_pairs={{0,32},{32,64},{64,96},{96,0},{1,33},{33,65},{65,97},{97,1},{2,34}... | collective-permute-start | bytes 1966088 | tf_op jit(solution)/shard_map/ppermute | solution.py:33
  70.6 17.4 %collective-permute-start.11 = (bf16[1280,256]{1,0:T(8,128)(2,1)}, bf16[1280,256]{1,0:T(8,128)(2,1)}, u32[]{:S(2)}, u32[]{:S(2)}) collective-permute-start(bf16[1280,256]{1,0:T(8,128)(2,1)} %collective-permute-done.10.refs_2_), channel_id=1, source_target_pairs={{0,96},{32,0},{64,32},{96,64},{1,97},{33,1},{65,33},{97,65},{2,98}... | collective-permute-start | bytes 1966088 | tf_op jit(solution)/shard_map/ppermute | solution.py:33
  77.1 25.9 %all-to-all-start.1 = ((bf16[16,64,512]{2,1,0:T(8,128)(2,1)}), bf16[16,64,512]{2,1,0:T(8,128)(2,1)}, u32[]{:S(2)}, u32[]{:S(2)}) async-start(bf16[16,64,512]{2,1,0:T(8,128)(2,1)} %bitcast.8), calls=%async_computation.1 | async-start | bytes 2097152 | tf_op jit(solution)/shard_map/all_to_all | solution.py:28
  103.0 56.3 %all-to-all-start.2 = ((bf16[16,80,512]{2,1,0:T(8,128)(2,1)}), bf16[16,80,512]{2,1,0:T(8,128)(2,1)}, u32[]{:S(2)}, u32[]{:S(2)}) async-start(bf16[16,80,512]{2,1,0:T(8,128)(2,1)} %bitcast.9), calls=%async_computation.2 | async-start | bytes 2621440 | tf_op jit(solution)/shard_map/all_to_all | solution.py:28
  108.3 20.0 %collective-permute-start.16 = (bf16[272,256]{1,0:T(8,128)(2,1)S(1)}, bf16[272,256]{1,0:T(8,128)(2,1)S(1)}, u32[]{:S(2)}, u32[]{:S(2)}) collective-permute-start(bf16[272,256]{1,0:T(8,128)(2,1)S(1)} %get-tuple-element.27), channel_id=1, source_target_pairs={{0,1},{1,2},{2,3},{3,0},{4,5},{5,6},{6,7},{7,4},{8,9},{9,10},{10,1... | collective-permute-start | bytes 417800 | tf_op jit(solution)/shard_map/ppermute | solution.py:33
  110.2 20.0 %collective-permute-start.17 = (bf16[272,256]{1,0:T(8,128)(2,1)S(1)}, bf16[272,256]{1,0:T(8,128)(2,1)S(1)}, u32[]{:S(2)}, u32[]{:S(2)}) collective-permute-start(bf16[272,256]{1,0:T(8,128)(2,1)S(1)} %get-tuple-element.27), channel_id=1, source_target_pairs={{0,2},{1,3},{2,0},{3,1},{4,6},{5,7},{6,4},{7,5},{8,10},{9,11},{10,... | collective-permute-start | bytes 417800 | tf_op jit(solution)/shard_map/ppermute | solution.py:33
  112.8 17.4 %collective-permute-start.18 = (bf16[272,256]{1,0:T(8,128)(2,1)S(1)}, bf16[272,256]{1,0:T(8,128)(2,1)S(1)}, u32[]{:S(2)}, u32[]{:S(2)}) collective-permute-start(bf16[272,256]{1,0:T(8,128)(2,1)S(1)} %get-tuple-element.27), channel_id=1, source_target_pairs={{0,3},{1,0},{2,1},{3,2},{4,7},{5,4},{6,5},{7,6},{8,11},{9,8},{10,9... | collective-permute-start | bytes 417800 | tf_op jit(solution)/shard_map/ppermute | solution.py:33
  130.3 26.8 %collective-permute-start.19 = (bf16[4,272,256]{2,1,0:T(8,128)(2,1)S(1)}, bf16[4,272,256]{2,1,0:T(8,128)(2,1)S(1)}, u32[]{:S(2)}, u32[]{:S(2)}) collective-permute-start(bf16[4,272,256]{2,1,0:T(8,128)(2,1)S(1)} %pad_maximum_fusion.refs_1_.refs_2_.refs_5_), channel_id=1, source_target_pairs={{0,4},{4,8},{8,12},{12,0},{1,5},{5,9},{9,13},{13,1},{2,6},{6,10},{... | collective-permute-start | bytes 1671176 | tf_op jit(solution)/shard_map/ppermute | solution.py:33
  131.8 17.6 %collective-permute-start.22 = (bf16[272,256]{1,0:T(8,128)(2,1)S(1)}, bf16[272,256]{1,0:T(8,128)(2,1)S(1)}, u32[]{:S(2)}, u32[]{:S(2)}) collective-permute-start(bf16[272,256]{1,0:T(8,128)(2,1)S(1)} %get-tuple-element.28), channel_id=1, source_target_pairs={{0,4},{4,8},{8,12},{12,0},{1,5},{5,9},{9,13},{13,1},{2,6},{6,10},{... | collective-permute-start | bytes 417800 | tf_op jit(solution)/shard_map/ppermute | solution.py:33
  133.3 20.6 %collective-permute-start.23 = (bf16[272,256]{1,0:T(8,128)(2,1)S(1)}, bf16[272,256]{1,0:T(8,128)(2,1)S(1)}, u32[]{:S(2)}, u32[]{:S(2)}) collective-permute-start(bf16[272,256]{1,0:T(8,128)(2,1)S(1)} %get-tuple-element.28), channel_id=1, source_target_pairs={{0,8},{4,12},{8,0},{12,4},{1,9},{5,13},{9,1},{13,5},{2,10},{6,14},... | collective-permute-start | bytes 417800 | tf_op jit(solution)/shard_map/ppermute | solution.py:33
  135.0 18.9 %collective-permute-start.24 = (bf16[272,256]{1,0:T(8,128)(2,1)S(1)}, bf16[272,256]{1,0:T(8,128)(2,1)S(1)}, u32[]{:S(2)}, u32[]{:S(2)}) collective-permute-start(bf16[272,256]{1,0:T(8,128)(2,1)S(1)} %get-tuple-element.28), channel_id=1, source_target_pairs={{0,12},{4,0},{8,4},{12,8},{1,13},{5,1},{9,5},{13,9},{2,14},{6,2},{... | collective-permute-start | bytes 417800 | tf_op jit(solution)/shard_map/ppermute | solution.py:33
  137.1 25.6 %collective-permute-start.20 = (bf16[4,272,256]{2,1,0:T(8,128)(2,1)S(1)}, bf16[4,272,256]{2,1,0:T(8,128)(2,1)S(1)}, u32[]{:S(2)}, u32[]{:S(2)}) collective-permute-start(bf16[4,272,256]{2,1,0:T(8,128)(2,1)S(1)} %pad_maximum_fusion.refs_1_.refs_2_.refs_5_), channel_id=1, source_target_pairs={{0,8},{4,12},{8,0},{12,4},{1,9},{5,13},{9,1},{13,5},{2,10},{6,14},... | collective-permute-start | bytes 1671176 | tf_op jit(solution)/shard_map/ppermute | solution.py:33
  149.4 16.3 %collective-permute-start.21 = (bf16[4,272,256]{2,1,0:T(8,128)(2,1)S(1)}, bf16[4,272,256]{2,1,0:T(8,128)(2,1)S(1)}, u32[]{:S(2)}, u32[]{:S(2)}) collective-permute-start(bf16[4,272,256]{2,1,0:T(8,128)(2,1)S(1)} %pad_maximum_fusion.refs_1_.refs_2_.refs_5_), channel_id=1, source_target_pairs={{0,12},{4,0},{8,4},{12,8},{1,13},{5,1},{9,5},{13,9},{2,14},{6,2},{... | collective-permute-start | bytes 1671176 | tf_op jit(solution)/shard_map/ppermute | solution.py:33
  154.0 22.7 %collective-permute-start.25 = (bf16[4,272,256]{2,1,0:T(8,128)(2,1)S(1)}, bf16[4,272,256]{2,1,0:T(8,128)(2,1)S(1)}, u32[]{:S(2)}, u32[]{:S(2)}) collective-permute-start(bf16[4,272,256]{2,1,0:T(8,128)(2,1)S(1)} %pad_maximum_fusion.1.refs_5_.refs_6_.refs_9_), channel_id=1, source_target_pairs={{0,1},{1,2},{2,3},{3,0},{4,5},{5,6},{6,7},{7,4},{8,9},{9,10},{10,1... | collective-permute-start | bytes 1671176 | tf_op jit(solution)/shard_map/ppermute | solution.py:33
  154.2 24.2 %collective-permute-start.26 = (bf16[4,272,256]{2,1,0:T(8,128)(2,1)S(1)}, bf16[4,272,256]{2,1,0:T(8,128)(2,1)}, u32[]{:S(2)}, u32[]{:S(2)}) collective-permute-start(bf16[4,272,256]{2,1,0:T(8,128)(2,1)S(1)} %pad_maximum_fusion.1.refs_5_.refs_6_.refs_9_), channel_id=1, source_target_pairs={{0,2},{1,3},{2,0},{3,1},{4,6},{5,7},{6,4},{7,5},{8,10},{9,11},{10,... | collective-permute-start | bytes 1671176 | tf_op jit(solution)/shard_map/ppermute | solution.py:33
  157.1 26.0 %collective-permute-start.27 = (bf16[4,272,256]{2,1,0:T(8,128)(2,1)S(1)}, bf16[4,272,256]{2,1,0:T(8,128)(2,1)}, u32[]{:S(2)}, u32[]{:S(2)}) collective-permute-start(bf16[4,272,256]{2,1,0:T(8,128)(2,1)S(1)} %pad_maximum_fusion.1.refs_5_.refs_6_.refs_9_), channel_id=1, source_target_pairs={{0,3},{1,0},{2,1},{3,2},{4,7},{5,4},{6,5},{7,6},{8,11},{9,8},{10,9... | collective-permute-start | bytes 1671176 | tf_op jit(solution)/shard_map/ppermute | solution.py:33
  162.8 15.7 %collective-permute-start.28 = (bf16[144,512]{1,0:T(8,128)(2,1)S(1)}, bf16[144,512]{1,0:T(8,128)(2,1)S(1)}, u32[]{:S(2)}, u32[]{:S(2)}) collective-permute-start(bf16[144,512]{1,0:T(8,128)(2,1)S(1)} %fusion.2.refs_9_), channel_id=1, source_target_pairs={{0,32},{32,64},{64,96},{96,0},{1,33},{33,65},{65,97},{97,1},{2,34}... | collective-permute-start | bytes 442376 | tf_op jit(solution)/shard_map/ppermute | solution.py:33
  165.6 13.3 %collective-permute-start.29 = (bf16[144,512]{1,0:T(8,128)(2,1)S(1)}, bf16[144,512]{1,0:T(8,128)(2,1)S(1)}, u32[]{:S(2)}, u32[]{:S(2)}) collective-permute-start(bf16[144,512]{1,0:T(8,128)(2,1)S(1)} %fusion.2.refs_9_), channel_id=1, source_target_pairs={{0,64},{32,96},{64,0},{96,32},{1,65},{33,97},{65,1},{97,33},{2,66}... | collective-permute-start | bytes 442376 | tf_op jit(solution)/shard_map/ppermute | solution.py:33
  191.3 10.1 %collective-permute-start.37 = (bf16[160,512]{1,0:T(8,128)(2,1)S(1)}, bf16[160,512]{1,0:T(8,128)(2,1)S(1)}, u32[]{:S(2)}, u32[]{:S(2)}) collective-permute-start(bf16[160,512]{1,0:T(8,128)(2,1)S(1)} %get-tuple-element.30.refs_10_), channel_id=1, source_target_pairs={{0,96},{32,0},{64,32},{96,64},{1,97},{33,1},{65,33},{97,65},{2,98}... | collective-permute-start | bytes 491528 | tf_op jit(solution)/shard_map/ppermute | solution.py:33
  191.5 9.9 %collective-permute-start.38 = (bf16[160,512]{1,0:T(8,128)(2,1)S(1)}, bf16[160,512]{1,0:T(8,128)(2,1)S(1)}, u32[]{:S(2)}, u32[]{:S(2)}) collective-permute-start(bf16[160,512]{1,0:T(8,128)(2,1)S(1)} %get-tuple-element.30.refs_10_), channel_id=1, source_target_pairs={{0,16},{16,0},{1,17},{17,1},{2,18},{18,2},{3,19},{19,3},{4,20},{20... | collective-permute-start | bytes 491528 | tf_op jit(solution)/shard_map/ppermute | solution.py:33
  208.8 10.2 %collective-permute-start.44 = (bf16[160,512]{1,0:T(8,128)(2,1)S(1)}, bf16[160,512]{1,0:T(8,128)(2,1)S(1)}, u32[]{:S(2)}, u32[]{:S(2)}) collective-permute-start(bf16[160,512]{1,0:T(8,128)(2,1)S(1)} %get-tuple-element.34.refs_13_), channel_id=1, source_target_pairs={{0,96},{32,0},{64,32},{96,64},{1,97},{33,1},{65,33},{97,65},{2,98}... | collective-permute-start | bytes 491528 | tf_op jit(solution)/shard_map/ppermute | solution.py:33
  236.4 28.1 %collective-permute-start.56 = (f32[144,256]{1,0:T(8,128)S(1)}, f32[144,256]{1,0:T(8,128)S(1)}, u32[]{:S(2)}, u32[]{:S(2)}) collective-permute-start(f32[144,256]{1,0:T(8,128)S(1)} %get-tuple-element.41), channel_id=1, source_target_pairs={{0,0},{1,1},{2,16},{3,17},{4,32},{5,33},{6,48},{7,49},{8,64},{9,65... | collective-permute-start | bytes 442376 | tf_op jit(solution)/shard_map/ppermute | solution.py:339
  250.8 13.7 %collective-permute-start.57 = (f32[144,256]{1,0:T(8,128)S(1)}, f32[144,256]{1,0:T(8,128)S(1)}, u32[]{:S(2)}, u32[]{:S(2)}) collective-permute-start(f32[144,256]{1,0:T(8,128)S(1)} %get-tuple-element.42), channel_id=1, source_target_pairs={{0,1},{1,0},{2,17},{3,16},{4,33},{5,32},{6,49},{7,48},{8,65},{9,64... | collective-permute-start | bytes 442376 | tf_op jit(solution)/shard_map/ppermute | solution.py:339
  (32 other events, 195.0 us)
